TPU v7x, 256 devices: a 4x2x16 block of a 4x16x16 slice. The times are simulated.
256 devices in a mesh: grp: 2 (over y), lon: 64 (over x, z), lat: 2 (over core).
Axes of the slice: x: 4, y: 2, z: 16, core: 2. Of those that a mesh axis runs over, the one named last changes fastest.
The devices are a block of a 4x16x16 slice.
Arguments:
- surface_field: bfloat16 [512, 512, 256], P(('grp', 'lat'), 'lon'), parts along dimension 0, may hold values from -6 to 6
- conv_a: bfloat16 [3, 3, 256, 512], replicated, may hold values from -0.125 to 0.125
- conv_b: bfloat16 [3, 3, 512, 512], replicated, may hold values from -0.09375 to 0.09375
- norm_gain: float32 [512], replicated, may hold values from 0.1 to 1.9
- qkv_weight: bfloat16 [512, 3072], replicated, may hold values from -3 to 3, as said below
- out_weight: bfloat16 [1024, 512], replicated, may hold values from -0.1875 to 0.1875
Outputs:
- mixed_out: bfloat16 [128, 128, 512], P(('grp', 'lat'), 'lon'), parts along dimension 0
There are 2 independent parts, one for each index of `grp`. A program takes and returns all parts, laid end to end along the dimension named above; an argument that names none is the same for every part. Nothing has to cross between parts.
Inputs may be any that keep to these rules, and one draw needn't show every extreme that they name: `qkv_weight`: columns hold queries, keys and values in that order, each 16 heads of 64 entries.
All inputs are finite; a program needn't handle non-finite values.
Results may differ from a plain program's by a relative error of at most 0.012.
The roundings to bfloat16 on the way count: a program that leaves them out, or rounds other values in their place, can miss the bound.
Values may be sent and summed in bfloat16 or wider, within the bound.
No kernel may reach another device: no remote copies, remote signals or barrier semaphores. Data moves between devices by JAX's collectives and lax.ppermute only.
A program may use at most 128 MiB of HBM per device.

v0:
```python
import jax
import jax.numpy as jnp
from jax import lax
from jax.sharding import PartitionSpec as P

CB = 512
HEADS = 16
HEAD_DIM = 64


def with_halo(block, sides, width):
    for axis, dim in sides:
        count = lax.axis_size(axis)
        forward = [(i, i + 1) for i in range(count - 1)]
        forward.append((count - 1, 0))
        backward = [(target, source) for source, target in forward]
        low = lax.ppermute(
            lax.slice_in_dim(block, block.shape[dim] - width, None, axis=dim), axis, forward
        )
        high = lax.ppermute(lax.slice_in_dim(block, 0, width, axis=dim), axis, backward)
        block = jnp.concatenate([low, block, high], axis=dim)
    return block


def partner_2(value, axis, distance):
    mask = 2**distance
    pairs = [(source, source ^ mask) for source in range(lax.axis_size(axis))]
    return lax.ppermute(value, axis, pairs)


def convolve(values_in, weight):
    return lax.conv_general_dilated(
        values_in[None],
        weight,
        (1, 1),
        "VALID",
        dimension_numbers=("NHWC", "HWIO", "NHWC"),
        preferred_element_type=jnp.float32,
    )[0]


def average_pool(values_in):
    rows_in, cols_in, chans_in = values_in.shape
    return values_in.reshape(rows_in // 2, 2, cols_in // 2, 2, chans_in).mean(axis=(1, 3))


def layer_norm(tokens_flat, norm_gain):
    centred = tokens_flat - jnp.mean(tokens_flat, axis=-1, keepdims=True)
    spread = jnp.mean(centred * centred, axis=-1, keepdims=True)
    return centred * lax.rsqrt(spread + 0.01) * norm_gain


def softmax_rows(scores):
    maxima = jnp.max(scores, axis=-1, keepdims=True)
    raised = jnp.exp(scores - maxima)
    return raised / jnp.sum(raised, axis=-1, keepdims=True)


def keep_rows(values_in, rows_here, lat_count, lat_where, margin):
    first_row = lat_where * rows_here - margin
    rowpos = first_row + jnp.arange(values_in.shape[0], dtype=jnp.int32)
    inside = (rowpos >= 0) & (rowpos < rows_here * lat_count)
    return jnp.where(inside[:, None, None], values_in, jnp.zeros((), values_in.dtype))


def body(surface_field, conv_a, conv_b, norm_gain, qkv_weight, out_weight):
    lon_count = lax.axis_size("lon")
    lat_count = lax.axis_size("lat")
    lat_where = lax.axis_index("lat")
    rows_here = surface_field.shape[0]
    padded_field = with_halo(surface_field, (("lon", 1), ("lat", 0)), 1)
    padded_field = keep_rows(padded_field, rows_here, lat_count, lat_where, 1)
    first_out = jax.nn.silu(convolve(padded_field, conv_a))
    pooled_first = average_pool(first_out).astype(jnp.bfloat16)
    ready_rows = with_halo(pooled_first, (("lon", 1), ("lat", 0)), 1)
    ready_rows = keep_rows(ready_rows, rows_here // 2, lat_count, lat_where, 1)
    second_out = jax.nn.silu(convolve(ready_rows, conv_b))
    pooled_second = average_pool(second_out)
    tok_rows, tok_cols = (pooled_second.shape[0], pooled_second.shape[1])
    local_tokens = tok_rows * tok_cols
    tokens_flat = pooled_second.reshape(local_tokens, CB)
    normed = layer_norm(tokens_flat, norm_gain).astype(jnp.bfloat16)
    projected = jnp.dot(normed, qkv_weight, preferred_element_type=jnp.float32).astype(jnp.bfloat16)
    residues = max(1, lon_count // HEADS)
    groups = lon_count // residues
    per_slot = HEADS // groups
    per_residue = local_tokens // residues
    arranged = projected.reshape(per_residue, residues, 3, groups, per_slot, HEAD_DIM)
    outgoing = arranged.transpose(2, 1, 3, 4, 0, 5).reshape(
        3, lon_count, per_slot, per_residue, HEAD_DIM
    )
    swap_bits = list(range(groups.bit_length() - 1, lon_count.bit_length() - 1))
    arrived = lax.all_to_all(outgoing, "lon", split_axis=1, concat_axis=3, tiled=True)
    queries = arrived[0, 0]
    keys_vals = arrived[1:, 0]
    for bit_pos in swap_bits:
        partner = partner_2(keys_vals, "lon", bit_pos)
        keys_vals = jnp.concatenate([keys_vals, partner], axis=2)
    bit_pos = 0
    partner = partner_2(keys_vals, "lat", bit_pos)
    keys_vals = jnp.concatenate([keys_vals, partner], axis=2)
    score_scale = HEAD_DIM ** (-0.5)
    scores = (
        jnp.einsum("hqd,hkd->hqk", queries, keys_vals[0], preferred_element_type=jnp.float32)
        * score_scale
    )
    weights = softmax_rows(scores).astype(jnp.bfloat16)
    head_out = jnp.einsum(
        "hqk,hkd->hqd", weights, keys_vals[1], preferred_element_type=jnp.float32
    ).astype(jnp.bfloat16)
    returned = lax.all_to_all(head_out[None], "lon", split_axis=2, concat_axis=0, tiled=True)
    attended = returned.reshape(residues, groups, per_slot, per_residue, HEAD_DIM).transpose(
        3, 0, 1, 2, 4
    )
    attended = attended.reshape(local_tokens, HEADS * HEAD_DIM)
    mixed_out = tokens_flat + jnp.dot(attended, out_weight, preferred_element_type=jnp.float32)
    return mixed_out.reshape(tok_rows, tok_cols, CB).astype(jnp.bfloat16)


def solution(mesh):
    in_specs = (P(("grp", "lat"), "lon", None), P(), P(), P(), P(), P())
    out_specs = P(("grp", "lat"), "lon", None)
    return jax.shard_map(body, mesh=mesh, in_specs=in_specs, out_specs=out_specs, check_vma=False)
```

profile of v0, /device:TPU:40, one launch (start us, length us, event | category | flops | bytes accessed | tf_op | source)
XLA Modules:
  0.0 236.8 jit_solution(10205431438477334216)
XLA Ops:
  0.0 2.2 fusion.19
  2.2 2.8 %collective-permute-start = (bf16[128,1,256]{2,1,0:T(2,128)(2,1)}, bf16[128,1,256]{2,1,0:T(2,128)(2,1)S(1)}, u32[]{:S(2)}, u32[]{:S(2)}) collective-permute-start(bf16[128,1,256]{2,1,0:T(2,128)(2,1)} %get-tuple-element.13), channel_id=1, source_target_pairs={{0,2},{2,4},{4,6},{6,8},{8,10},{10,12},{12,14},{14,16},{16,18},{18... | collective-permute-start | bytes 196616 | tf_op jit(solution)/shard_map/ppermute | solution.py:17
  5.0 22.2 %collective-permute-start.1 = (bf16[128,1,256]{2,1,0:T(2,128)(2,1)S(1)}, bf16[128,1,256]{2,1,0:T(2,128)(2,1)S(1)}, u32[]{:S(2)}, u32[]{:S(2)}) collective-permute-start(bf16[128,1,256]{2,1,0:T(2,128)(2,1)S(1)} %get-tuple-element.14), channel_id=1, source_target_pairs={{2,0},{4,2},{6,4},{8,6},{10,8},{12,10},{14,12},{16,14},{18,16},{20... | collective-permute-start | bytes 196616 | tf_op jit(solution)/shard_map/ppermute | solution.py:20
  27.2 3.8 %collective-permute-done = bf16[128,1,256]{2,1,0:T(2,128)(2,1)S(1)} collective-permute-done((bf16[128,1,256]{2,1,0:T(2,128)(2,1)}, bf16[128,1,256]{2,1,0:T(2,128)(2,1)S(1)}, u32[]{:S(2)}, u32[]{:S(2)}) %collective-permute-start) | collective-permute-done | bytes 65568 | tf_op jit(solution)/shard_map/ppermute | solution.py:17
  31.0 1.8 fusion.16
  32.7 0.1 collective-permute-start.2
  32.9 0.7 collective-permute-start.3
  33.5 0.5 collective-permute-done.2
  34.0 0.3 collective-permute-done.3
  34.4 0.3 maximum_select_fusion
  34.6 19.4 %convolution_reduce_fusion = f32[128,8,512]{2,1,0:T(8,128)} fusion(bf16[3,3,256,512]{3,2,1,0:T(8,128)(2,1)S(1)} %copy-done.4, bf16[1,130,10,256]{3,2,1,0:T(8,128)(2,1)S(1)} %maximum_select_fusion), kind=kOutput, calls=%fused_computation.9 | convolution fusion | flops 2415919104 | bytes 5122048 | tf_op jit(solution)/shard_map/conv_general_dilated | solution.py:32
  54.0 3.5 %squeeze.12 = f32[64,2,4,2,512]{4,3,2,1,0:T(2,128)} reshape(f32[128,8,512]{2,1,0:T(8,128)} %convolution_reduce_fusion) | data formatting | bytes 4194304 | tf_op jit(solution)/shard_map/squeeze | solution.py:32
  57.5 4.8 %fusion.2 = f32[64,4,512]{2,1,0:T(4,128)S(1)} fusion(f32[64,2,4,2,512]{4,3,2,1,0:T(2,128)} %squeeze.12), kind=kLoop, calls=%fused_computation.8 | loop fusion | flops 2490368 | bytes 2621440 | tf_op jit(solution)/shard_map/reduce_sum | solution.py:44
  62.3 0.1 multiply_convert_fusion
  62.4 0.9 fusion.20
  63.3 0.4 collective-permute-start.4
  63.7 5.3 %collective-permute-start.5 = (bf16[64,1,512]{2,1,0:T(2,128)(2,1)}, bf16[64,1,512]{2,1,0:T(2,128)(2,1)}, u32[]{:S(2)}, u32[]{:S(2)}) collective-permute-start(bf16[64,1,512]{2,1,0:T(2,128)(2,1)} %get-tuple-element.16), channel_id=1, source_target_pairs={{2,0},{4,2},{6,4},{8,6},{10,8},{12,10},{14,12},{16,14},{18,16},{20... | collective-permute-start | bytes 196616 | tf_op jit(solution)/shard_map/ppermute | solution.py:20
  69.0 3.9 %collective-permute-done.4 = bf16[64,1,512]{2,1,0:T(2,128)(2,1)S(1)} collective-permute-done((bf16[64,1,512]{2,1,0:T(2,128)(2,1)}, bf16[64,1,512]{2,1,0:T(2,128)(2,1)S(1)}, u32[]{:S(2)}, u32[]{:S(2)}) %collective-permute-start.4) | collective-permute-done | bytes 65568 | tf_op jit(solution)/shard_map/ppermute | solution.py:17
  73.0 1.3 fusion.15
  74.3 0.1 collective-permute-start.6
  74.5 0.5 collective-permute-start.7
  75.0 0.7 collective-permute-done.6
  75.6 0.2 collective-permute-done.7
  75.8 0.2 maximum_select_fusion.1
  76.0 12.1 %convolution_reduce_fusion.1 = f32[64,4,512]{2,1,0:T(4,128)} fusion(bf16[3,3,512,512]{3,2,1,0:T(8,128)(2,1)} %param.8, bf16[1,66,6,512]{3,2,1,0:T(8,128)(2,1)S(1)} %maximum_select_fusion.1), kind=kOutput, calls=%fused_computation.11 | convolution fusion | flops 1207959552 | bytes 5648384 | tf_op jit(solution)/shard_map/conv_general_dilated | solution.py:32
  88.1 2.3 squeeze.13
  90.3 2.0 fusion.9
  92.3 0.1 fusion.14
  92.5 0.2 multiply_reduce_fusion.1
  92.7 0.1 div.57
  92.8 0.7 div.55
  93.6 0.1 rsqrt.12
  93.7 1.6 convolution_convert_fusion
  95.3 0.5 reshape.199
  95.8 0.5 copy.23
  96.3 0.1 copy.41
  96.5 0.5 reshape.208
  97.0 34.1 %all_to_all.8 = bf16[64,2,1536]{2,1,0:T(2,128)(2,1)S(1)} all-to-all(bf16[64,2,1536]{2,1,0:T(2,128)(2,1)S(1)} %reshape.208), channel_id=1, replica_groups=mesh['grp'=2,'lon'=64,'lat'=2] {'lon'}, dimensions={0} | all-to-all | bytes 786432 | tf_op jit(solution)/shard_map/all_to_all | solution.py:93
  131.1 0.5 reshape.209
  131.7 1.5 collective-permute-start.8
  133.2 10.4 %collective-permute-done.8 = bf16[2,1,1024,64]{3,2,0,1:T(8,128)(2,1)S(1)} collective-permute-done((bf16[2,1,1024,64]{3,2,0,1:T(8,128)(2,1)S(1)}, bf16[2,1,1024,64]{3,2,0,1:T(8,128)(2,1)S(1)}, u32[]{:S(2)}, u32[]{:S(2)}) %collective-permute-start.8) | collective-permute-done | bytes 262176 | tf_op jit(solution)/shard_map/ppermute | solution.py:28
  143.6 0.2 pad_maximum_fusion.2
  143.8 1.1 copy.26
  144.9 3.1 %collective-permute-start.9 = (bf16[2,1,2048,64]{2,3,1,0:T(8,128)(2,1)}, bf16[2,1,2048,64]{2,3,1,0:T(8,128)(2,1)S(1)}, u32[]{:S(2)}, u32[]{:S(2)}) collective-permute-start(bf16[2,1,2048,64]{2,3,1,0:T(8,128)(2,1)} %copy.26), channel_id=1, source_target_pairs={{0,64},{2,66},{4,68},{6,70},{8,72},{10,74},{12,76},{14,78},{16,80}... | collective-permute-start | bytes 1572872 | tf_op jit(solution)/shard_map/ppermute | solution.py:28
  148.0 0.2 copy.29
  148.2 0.2 copy.30
  148.4 9.2 %collective-permute-done.9 = bf16[2,1,2048,64]{2,3,1,0:T(8,128)(2,1)S(1)} collective-permute-done((bf16[2,1,2048,64]{2,3,1,0:T(8,128)(2,1)}, bf16[2,1,2048,64]{2,3,1,0:T(8,128)(2,1)S(1)}, u32[]{:S(2)}, u32[]{:S(2)}) %collective-permute-start.9) | collective-permute-done | bytes 524320 | tf_op jit(solution)/shard_map/ppermute | solution.py:28
  157.6 0.1 pad_maximum_fusion.3
  157.7 0.1 collective-permute-start.10
  157.9 2.6 %collective-permute-done.10 = bf16[2,1,4096,64]{2,3,1,0:T(8,128)(2,1)S(1)} collective-permute-done((bf16[2,1,4096,64]{2,3,1,0:T(8,128)(2,1)S(1)}, bf16[2,1,4096,64]{2,3,1,0:T(8,128)(2,1)S(1)}, u32[]{:S(2)}, u32[]{:S(2)}) %collective-permute-start.10) | collective-permute-done | bytes 1048608 | tf_op jit(solution)/shard_map/ppermute | solution.py:28
  160.5 0.1 pad_maximum_fusion
  160.6 13.0 %multiply_reduce_fusion = (f32[1024]{0:T(1024)S(1)}, f32[1024,8192]{1,0:T(8,128)}) fusion(bf16[1024,64]{1,0:T(8,128)(2,1)S(1)} %bitcast.51, bf16[2,1,8192,64]{2,3,1,0:T(8,128)(2,1)S(1)} %pad_maximum_fusion), kind=kOutput, calls=%fused_computation.2 | convolution fusion | flops 1090518016 | bytes 34869248 | tf_op jit(solution)/shard_map/hqd,hkd->hqk/dot_general | solution.py:104
  173.7 14.1 %fusion = f32[1024]{0:T(1024)S(1)} fusion(f32[1024,8192]{1,0:T(8,128)} %get-tuple-element.20, f32[1024]{0:T(1024)S(1)} %get-tuple-element.19), kind=kLoop, calls=%fused_computation.3 | loop fusion | flops 25164800 | bytes 33562624 | tf_op jit(solution)/shard_map/reduce_sum | solution.py:56
  187.7 13.3 %fusion.5 = bf16[1,1,1024,64]{2,3,1,0:T(8,128)(2,1)S(1)} fusion(f32[1024,8192]{1,0:T(8,128)} %get-tuple-element.20, f32[1024]{0:T(1024)S(1)} %fusion, f32[1024]{0:T(1024)S(1)} %get-tuple-element.19, bf16[2,1,8192,64]{2,3,1,0:T(8,128)(2,1)S(1)} %pad_maximum_fusion), kind=kOutput, calls=%fused_computation.14 | convolution fusion | flops 1107361792 | bytes 34742272 | tf_op jit(solution)/shard_map/hqk,hkd->hqd/dot_general | solution.py:108
  201.0 0.4 copy.31
  201.4 0.5 broadcast.124
  201.9 2.3 reduce.10
  204.2 0.8 reshape.210
  205.0 26.3 %all_to_all.9 = bf16[64,2,512]{2,1,0:T(2,128)(2,1)S(1)} all-to-all(bf16[64,2,512]{2,1,0:T(2,128)(2,1)} %reshape.210), channel_id=1, replica_groups=mesh['grp'=2,'lon'=64,'lat'=2] {'lon'}, dimensions={0} | all-to-all | bytes 262144 | tf_op jit(solution)/shard_map/all_to_all | solution.py:111
  231.4 1.0 reshape.211
  232.4 1.1 copy.35
  233.5 0.8 reshape.205
  234.4 1.6 fusion.6
  236.0 0.7 convert_element_type.29
  (22 shorter events, 0.2 us)
Async XLA Ops:
  0.0 93.7 %copy-start = (bf16[512,3072]{1,0:T(8,128)(2,1)S(1)}, bf16[512,3072]{1,0:T(8,128)(2,1)}, u32[]{:S(2)}) copy-start(bf16[512,3072]{1,0:T(8,128)(2,1)} %param.10) | copy-start | bytes 9437188
  2.2 28.8 %collective-permute-start = (bf16[128,1,256]{2,1,0:T(2,128)(2,1)}, bf16[128,1,256]{2,1,0:T(2,128)(2,1)S(1)}, u32[]{:S(2)}, u32[]{:S(2)}) collective-permute-start(bf16[128,1,256]{2,1,0:T(2,128)(2,1)} %get-tuple-element.13), channel_id=1, source_target_pairs={{0,2},{2,4},{4,6},{6,8},{8,10},{10,12},{12,14},{14,16},{16,18},{18... | collective-permute-start | bytes 196616 | tf_op jit(solution)/shard_map/ppermute | solution.py:17
  5.0 26.0 %collective-permute-start.1 = (bf16[128,1,256]{2,1,0:T(2,128)(2,1)S(1)}, bf16[128,1,256]{2,1,0:T(2,128)(2,1)S(1)}, u32[]{:S(2)}, u32[]{:S(2)}) collective-permute-start(bf16[128,1,256]{2,1,0:T(2,128)(2,1)S(1)} %get-tuple-element.14), channel_id=1, source_target_pairs={{2,0},{4,2},{6,4},{8,6},{10,8},{12,10},{14,12},{16,14},{18,16},{20... | collective-permute-start | bytes 196616 | tf_op jit(solution)/shard_map/ppermute | solution.py:20
  27.2 7.4 %copy-start.4 = (bf16[3,3,256,512]{3,2,1,0:T(8,128)(2,1)S(1)}, bf16[3,3,256,512]{3,2,1,0:T(8,128)(2,1)}, u32[]{:S(2)}) copy-start(bf16[3,3,256,512]{3,2,1,0:T(8,128)(2,1)} %param.7) | copy-start | bytes 7077892
  32.7 1.3 collective-permute-start.2
  32.9 1.5 collective-permute-start.3
  63.3 9.7 %collective-permute-start.4 = (bf16[64,1,512]{2,1,0:T(2,128)(2,1)}, bf16[64,1,512]{2,1,0:T(2,128)(2,1)S(1)}, u32[]{:S(2)}, u32[]{:S(2)}) collective-permute-start(bf16[64,1,512]{2,1,0:T(2,128)(2,1)} %get-tuple-element.15), channel_id=1, source_target_pairs={{0,2},{2,4},{4,6},{6,8},{8,10},{10,12},{12,14},{14,16},{16,18},{18... | collective-permute-start | bytes 196616 | tf_op jit(solution)/shard_map/ppermute | solution.py:17
  63.7 9.3 %collective-permute-start.5 = (bf16[64,1,512]{2,1,0:T(2,128)(2,1)}, bf16[64,1,512]{2,1,0:T(2,128)(2,1)}, u32[]{:S(2)}, u32[]{:S(2)}) collective-permute-start(bf16[64,1,512]{2,1,0:T(2,128)(2,1)} %get-tuple-element.16), channel_id=1, source_target_pairs={{2,0},{4,2},{6,4},{8,6},{10,8},{12,10},{14,12},{16,14},{18,16},{20... | collective-permute-start | bytes 196616 | tf_op jit(solution)/shard_map/ppermute | solution.py:20
  74.3 1.3 collective-permute-start.6
  74.5 1.3 collective-permute-start.7
  88.1 5.6 %copy-start.3 = (f32[512]{0:T(512)S(1)}, f32[512]{0:T(512)}, u32[]{:S(2)}) copy-start(f32[512]{0:T(512)} %param.9) | copy-start | bytes 6148
  131.7 11.9 %collective-permute-start.8 = (bf16[2,1,1024,64]{3,2,0,1:T(8,128)(2,1)S(1)}, bf16[2,1,1024,64]{3,2,0,1:T(8,128)(2,1)S(1)}, u32[]{:S(2)}, u32[]{:S(2)}) collective-permute-start(bf16[2,1,1024,64]{3,2,0,1:T(8,128)(2,1)S(1)} %bitcast.42), channel_id=1, source_target_pairs={{0,32},{2,34},{4,36},{6,38},{8,40},{10,42},{12,44},{14,46},{16,48}... | collective-permute-start | bytes 786440 | tf_op jit(solution)/shard_map/ppermute | solution.py:28
  144.9 12.7 %collective-permute-start.9 = (bf16[2,1,2048,64]{2,3,1,0:T(8,128)(2,1)}, bf16[2,1,2048,64]{2,3,1,0:T(8,128)(2,1)S(1)}, u32[]{:S(2)}, u32[]{:S(2)}) collective-permute-start(bf16[2,1,2048,64]{2,3,1,0:T(8,128)(2,1)} %copy.26), channel_id=1, source_target_pairs={{0,64},{2,66},{4,68},{6,70},{8,72},{10,74},{12,76},{14,78},{16,80}... | collective-permute-start | bytes 1572872 | tf_op jit(solution)/shard_map/ppermute | solution.py:28
  157.7 2.8 %collective-permute-start.10 = (bf16[2,1,4096,64]{2,3,1,0:T(8,128)(2,1)S(1)}, bf16[2,1,4096,64]{2,3,1,0:T(8,128)(2,1)S(1)}, u32[]{:S(2)}, u32[]{:S(2)}) collective-permute-start(bf16[2,1,4096,64]{2,3,1,0:T(8,128)(2,1)S(1)} %pad_maximum_fusion.3), channel_id=1, source_target_pairs={{0,1},{1,0},{2,3},{3,2},{4,5},{5,4},{6,7},{7,6},{8,9},{9,8},{10,11... | collective-permute-start | bytes 3145736 | tf_op jit(solution)/shard_map/ppermute | solution.py:28
  201.0 33.4 %copy-start.2 = (f32[64,512]{1,0:T(8,128)S(1)}, f32[64,512]{1,0:T(8,128)}, u32[]{:S(2)}) copy-start(f32[64,512]{1,0:T(8,128)} %div.55) | copy-start | bytes 393220
  204.2 32.5 %copy-start.1 = (bf16[512,3072]{1,0:T(8,128)(2,1)S(1)}, bf16[512,3072]{1,0:T(8,128)(2,1)}, u32[]{:S(2)}) copy-start(bf16[512,3072]{1,0:T(8,128)(2,1)} %param.10) | copy-start | bytes 9437188
where the time goes:
time: 241 us; the launch traced here: 237 us
  matrix products  61 us (25%)
  blocking collectives  60.5 us (25%)
  starting transfers between devices  36.9 us (15%)
  waiting for transfers between devices  31.6 us (13%)
  other arithmetic  27.6 us (11%)
  local copies, waits for them, and re-layouts  18.8 us (8%)
    all_to_all x1, blocking collectives, body(): lax.all_to_all(outgoing, 'lon', split_axis=1, concat_axis=3, tiled=True)  34.1 us
    conv_general_dilated x2, matrix products, convolve(): lax.conv_general_dilated(values_in[None], weight, (1, 1), 'VALID', dimens...  31.5 us
    ppermute x4, starting transfers between devices, with_halo(): lax.ppermute(lax.slice_in_dim(block, 0, width, axis=dim), axis, backward)  28.7 us
    all_to_all x1, blocking collectives, body(): lax.all_to_all(head_out[None], 'lon', split_axis=2, concat_axis=0, tiled=...  26.3 us
    ppermute x3, waiting for transfers between devices, partner_2(): return lax.ppermute(value, axis, pairs)  22.2 us
    reduce_sum x1, other arithmetic, softmax_rows(): return raised / jnp.sum(raised, axis=-1, keepdims=True)  14.1 us
    dot_general x1, matrix products, body(): jnp.einsum('hqk,hkd->hqd', weights, keys_vals[1], preferred_element_type=...  13.3 us
    dot_general x1, matrix products, body(): jnp.einsum('hqd,hkd->hqk', queries, keys_vals[0], preferred_element_type=...  13 us
  transfers between devices with their start and end apart: 11, of which 9 were waited for; matrix products, arithmetic and copies ran while one was open for 0% of the time, Pallas kernels for 0%

commit v1 on v0

v1 whole, which is shorter than its diff:
```python
import functools
import math

import jax
import jax.numpy as jnp
from jax import lax
from jax.experimental import pallas as pl
from jax.experimental.pallas import tpu as pltpu
from jax.sharding import PartitionSpec as P

CB = 512
HEADS = 16
HEAD_DIM = 64
REACH = 3
BF = jnp.bfloat16
F32 = jnp.float32
VMEM = pl.BlockSpec(memory_space=pltpu.VMEM)
SMEM = pl.BlockSpec(memory_space=pltpu.SMEM)
HBM = pl.BlockSpec(memory_space=pltpu.HBM)


def silu(v):
    half = 0.5 * v
    return half + half * jnp.tanh(half)


def lanes_of(shape):
    return lax.broadcasted_iota(jnp.int32, shape, len(shape) - 1)


def conv_kernel(
    lat_ref, mid_ref, low_ref, high_ref, lat_mid_ref, lat_low_ref, lat_high_ref, gain_ref,
    conv_a_hbm, conv_b_hbm, qkv_hbm,
    tok_ref, out_ref,
    conv_a_ref, conv_b_ref, qkv_ref, wide, shifted, pool_a, ready, pool_b, sems,
):
    copies = [
        pltpu.make_async_copy(conv_a_hbm, conv_a_ref, sems.at[0]),
        pltpu.make_async_copy(conv_b_hbm, conv_b_ref, sems.at[1]),
        pltpu.make_async_copy(qkv_hbm, qkv_ref, sems.at[2]),
    ]
    for copy in copies:
        copy.start()
    lat = lat_ref[0]
    last = lat_ref[1] - 1
    cols, rows, chans = mid_ref.shape
    span = shifted.shape[2]
    for ref, edge, at in (
        (low_ref, lat_low_ref, 0),
        (mid_ref, lat_mid_ref, REACH),
        (high_ref, lat_high_ref, REACH + cols),
    ):
        n = ref.shape[0]
        wide[at : at + n, REACH : REACH + rows, :] = ref[...].astype(F32)
        rows_edge = edge[...].astype(F32)
        nothing = jnp.zeros_like(rows_edge)
        wide[at : at + n, 0:REACH, :] = jnp.where(lat == 0, nothing, rows_edge)
        wide[at : at + n, REACH + rows : 2 * REACH + rows, :] = jnp.where(
            lat == last, nothing, rows_edge
        )
    tail = 2 * REACH + rows
    wide[:, tail:, :] = jnp.zeros((wide.shape[0], wide.shape[1] - tail, chans), F32)
    for a in range(3):
        shifted[a] = wide[:, a : a + span, :].astype(BF)
    copies[0].wait()
    slabs = CB // 128
    pooled_cols = cols // 2 + 2
    for c in range(pooled_cols):
        parts = [
            shifted[a, 2 * c + b : 2 * c + b + 2].reshape(2 * span, chans)
            for a in range(3)
            for b in range(3)
        ]
        first = silu(
            jnp.dot(jnp.concatenate(parts, axis=1), conv_a_ref[...], preferred_element_type=F32)
        )
        pair = first[:span] + first[span:]
        for s in range(slabs):
            pool_a[c * slabs + s] = pair[:, 128 * s : 128 * (s + 1)]
    pooled_rows = rows // 2

    @pl.when(lat == 0)
    def _():
        pool_a[:, 0:2, :] = jnp.zeros((pool_a.shape[0], 2, 128), F32)

    @pl.when(lat == last)
    def _():
        pool_a[:, rows + 2 : rows + 4, :] = jnp.zeros((pool_a.shape[0], 2, 128), F32)

    for c in range(pooled_cols):
        for s in range(slabs):
            for a in range(3):
                even = pool_a[c * slabs + s, pl.ds(2 * a, pooled_rows, stride=2), :]
                odd = pool_a[c * slabs + s, pl.ds(2 * a + 1, pooled_rows, stride=2), :]
                ready[a, c, :, 128 * s : 128 * (s + 1)] = ((even + odd) * 0.25).astype(BF)
    copies[1].wait()
    cols_b = cols // 2
    parts = [
        ready[a, b : b + cols_b].reshape(cols_b * pooled_rows, CB)
        for a in range(3)
        for b in range(3)
    ]
    second = silu(
        jnp.dot(jnp.concatenate(parts, axis=1), conv_b_ref[...], preferred_element_type=F32)
    )
    tokens = []
    for c in range(cols_b // 2):
        at = 2 * c * pooled_rows
        pair = second[at : at + pooled_rows] + second[at + pooled_rows : at + 2 * pooled_rows]
        pieces = []
        for s in range(slabs):
            pool_b[c * slabs + s] = pair[:, 128 * s : 128 * (s + 1)]
            even = pool_b[c * slabs + s, pl.ds(0, pooled_rows // 2, stride=2), :]
            odd = pool_b[c * slabs + s, pl.ds(1, pooled_rows // 2, stride=2), :]
            pieces.append((even + odd) * 0.25)
        tokens.append(jnp.concatenate(pieces, axis=1))
    tokens = jnp.concatenate(tokens, axis=0)
    tok_ref[...] = tokens
    centred = tokens - jnp.mean(tokens, axis=-1, keepdims=True)
    spread = jnp.mean(centred * centred, axis=-1, keepdims=True)
    normed = (centred * lax.rsqrt(spread + 0.01) * gain_ref[...]).astype(BF)
    copies[2].wait()
    width = HEADS * HEAD_DIM
    count = tokens.shape[0]
    half = count // 2
    projected = jnp.dot(normed, qkv_ref[...], preferred_element_type=F32)
    below = lanes_of((count, 128)) < HEAD_DIM
    below_half = lanes_of((half, 128)) < HEAD_DIM
    for pair in range(HEADS // 2):
        q, k, v = (
            projected[:, width * s + 128 * pair : width * s + 128 * (pair + 1)] for s in range(3)
        )
        turned = [pltpu.roll(x, HEAD_DIM, 1) for x in (q, k, v)]
        h = 2 * pair
        out_ref[h, :count] = jnp.where(below, k, turned[2]).astype(BF)
        out_ref[h + 1, :count] = jnp.where(below, turned[1], v).astype(BF)
        out_ref[h, count:] = jnp.where(below_half, q[:half], turned[0][half:]).astype(BF)
        out_ref[h + 1, count:] = jnp.where(below_half, turned[0][:half], q[half:]).astype(BF)


def attention_kernel(q_ref, *refs):
    kv_refs, (out_ref, queries, ones_vals) = refs[:-3], refs[-3:]
    packed_rows = q_ref.shape[0]
    keys = kv_refs[0].shape[0]
    packed = q_ref[...].astype(F32)
    below = lanes_of((packed_rows, 128)) < HEAD_DIM
    zero = jnp.zeros_like(packed)
    queries[0] = jnp.where(below, packed, zero).astype(BF)
    queries[1] = jnp.where(below, pltpu.roll(packed, HEAD_DIM, 1), zero).astype(BF)
    one = jnp.ones((keys, 128), BF)
    below_keys = lanes_of((keys, 128)) < HEAD_DIM
    for i, kv in enumerate(kv_refs):
        ones_vals[i] = jnp.where(below_keys, one, kv[...])
    factor = HEAD_DIM ** (-0.5) * math.log2(math.e)
    block = 128

    def step(j, carry):
        at = pl.multiple_of(j * block, block)
        q = queries[:, pl.ds(at, block), :].reshape(2 * block, 128)
        top = jnp.full((2 * block, 1), -jnp.inf, F32)
        acc = jnp.zeros((2 * block, 128), F32)
        for i, kv in enumerate(kv_refs):
            scores = lax.dot_general(
                q, kv[...], (((1,), (1,)), ((), ())), preferred_element_type=F32
            )
            new_top = jnp.maximum(top, jnp.max(scores, axis=-1, keepdims=True))
            raised = jnp.exp2((scores - new_top) * factor).astype(BF)
            part = jnp.dot(raised, ones_vals[i], preferred_element_type=F32)
            acc = part if i == 0 else acc * jnp.exp2((top - new_top) * factor) + part
            top = new_top
        turned = pltpu.roll(acc, HEAD_DIM, 1)
        low = turned[:block] / acc[:block]
        high = acc[block:] / turned[block:]
        mask = lanes_of((block, 128)) < HEAD_DIM
        out_ref[pl.ds(at, block), :] = jnp.where(mask, low, high).astype(BF)
        return carry

    lax.fori_loop(0, packed_rows // block, step, 0)


def out_kernel(back_ref, tok_ref, weight_ref, out_ref):
    half = back_ref.shape[1]
    low, high = [], []
    mask = lanes_of((half, 128)) < HEAD_DIM
    for pair in range(HEADS // 2):
        even = back_ref[2 * pair].astype(F32)
        odd = back_ref[2 * pair + 1].astype(F32)
        low.append(jnp.where(mask, even, pltpu.roll(odd, HEAD_DIM, 1)).astype(BF))
        high.append(jnp.where(mask, pltpu.roll(even, HEAD_DIM, 1), odd).astype(BF))
    attended = jnp.concatenate(
        [jnp.concatenate(low, axis=1), jnp.concatenate(high, axis=1)], axis=0
    )
    mixed = tok_ref[...] + jnp.dot(attended, weight_ref[...], preferred_element_type=F32)
    out_ref[...] = mixed.astype(BF)


def body(surface_field, conv_a, conv_b, norm_gain, qkv_weight, out_weight):
    lon_count = lax.axis_size("lon")
    lat_count = lax.axis_size("lat")
    lat = lax.axis_index("lat")
    rows, cols, chans = surface_field.shape
    field = surface_field.transpose(1, 0, 2)
    forward = [(i, (i + 1) % lon_count) for i in range(lon_count)]
    backward = [(target, source) for source, target in forward]

    def across(pairs):
        return [
            (s * lat_count + c, t * lat_count + (c + 1) % lat_count)
            for s, t in pairs
            for c in range(lat_count)
        ]

    swap = [(c, (c + 1) % lat_count) for c in range(lat_count)]
    edge = jnp.where(lat == 0, field[:, rows - REACH :], field[:, :REACH])
    low = lax.ppermute(field[cols - REACH :], "lon", forward)
    high = lax.ppermute(field[:REACH], "lon", backward)
    lat_mid = lax.ppermute(edge, "lat", swap)
    lat_low = lax.ppermute(edge[cols - REACH :], ("lon", "lat"), across(forward))
    lat_high = lax.ppermute(edge[:REACH], ("lon", "lat"), across(backward))

    wide_cols = cols + 2 * REACH
    span = -(-(rows + 4) // 16) * 16
    pooled_cols = cols // 2 + 2
    pooled_rows = rows // 2
    count = (rows // 4) * (cols // 4)
    half = count // 2
    slabs = CB // 128
    where = jnp.stack([lat, jnp.int32(lat_count)]).astype(jnp.int32)
    tokens, outgoing = pl.pallas_call(
        conv_kernel,
        out_shape=(
            jax.ShapeDtypeStruct((count, CB), F32),
            jax.ShapeDtypeStruct((HEADS, count + half, 128), BF),
        ),
        in_specs=[SMEM] + [VMEM] * 7 + [HBM] * 3,
        out_specs=(VMEM, VMEM),
        scratch_shapes=[
            pltpu.VMEM((9 * chans, CB), BF),
            pltpu.VMEM((9 * CB, CB), BF),
            pltpu.VMEM(qkv_weight.shape, BF),
            pltpu.VMEM((wide_cols, span + 8, chans), F32),
            pltpu.VMEM((3, wide_cols, span, chans), BF),
            pltpu.VMEM((pooled_cols * slabs, span, 128), F32),
            pltpu.VMEM((3, pooled_cols, pooled_rows, CB), BF),
            pltpu.VMEM((cols // 4 * slabs, pooled_rows, 128), F32),
            pltpu.SemaphoreType.DMA((3,)),
        ],
        compiler_params=pltpu.CompilerParams(vmem_limit_bytes=40 * 2**20),
        name="convs",
    )(
        where, field, low, high, lat_mid, lat_low, lat_high, norm_gain.reshape(1, CB),
        conv_a.reshape(9 * chans, CB), conv_b.reshape(9 * CB, CB), qkv_weight,
    )

    residues = lon_count // HEADS
    groups = [[r * HEADS + h for h in range(HEADS)] for r in range(residues)]
    arrived = lax.all_to_all(outgoing, "lon", 0, 0, axis_index_groups=groups, tiled=True)
    queries = arrived[:, count:].reshape(HEADS * half, 128)
    own = arrived[:, :count].reshape(HEADS * count, 128)
    pieces = [own]
    for d in range(1, residues):
        pairs = [
            (r * HEADS + h, (r + d) % residues * HEADS + h)
            for r in range(residues)
            for h in range(HEADS)
        ]
        pieces.append(lax.ppermute(own, "lon", pairs))
    pieces += [lax.ppermute(piece, "lat", swap) for piece in pieces]
    attended = pl.pallas_call(
        attention_kernel,
        out_shape=jax.ShapeDtypeStruct((HEADS * half, 128), BF),
        in_specs=[VMEM] * (1 + len(pieces)),
        out_specs=VMEM,
        scratch_shapes=[
            pltpu.VMEM((2, HEADS * half, 128), BF),
            pltpu.VMEM((len(pieces), HEADS * count, 128), BF),
        ],
        compiler_params=pltpu.CompilerParams(vmem_limit_bytes=40 * 2**20),
        name="attention",
    )(queries, *pieces)
    returned = lax.all_to_all(
        attended.reshape(HEADS, half, 128), "lon", 0, 0, axis_index_groups=groups, tiled=True
    )
    mixed = pl.pallas_call(
        out_kernel,
        out_shape=jax.ShapeDtypeStruct((count, CB), BF),
        in_specs=[VMEM] * 3,
        out_specs=VMEM,
        name="mix",
    )(returned, tokens, out_weight)
    return mixed.reshape(cols // 4, rows // 4, CB).transpose(1, 0, 2)


def solution(mesh):
    in_specs = (P(("grp", "lat"), "lon", None), P(), P(), P(), P(), P())
    out_specs = P(("grp", "lat"), "lon", None)
    return jax.shard_map(body, mesh=mesh, in_specs=in_specs, out_specs=out_specs, check_vma=False)
```

time: 241 us -> 139 us (0.58); the launches traced: 237 us -> 139 us
  matrix products: 61 us -> 0 us
  other arithmetic: 27.6 us -> 0.09 us
  Pallas kernels: 0 us -> 27.3 us
  waiting for transfers between devices: 31.6 us -> 18.3 us
  local copies, waits for them, and re-layouts: 18.8 us -> 9.31 us
  blocking collectives: 60.5 us -> 51.3 us
  starting transfers between devices: 36.9 us -> 32.2 us
    conv_general_dilated x2 -> x0, matrix products: 31.5 us -> none  [convolve(): lax.conv_general_dilated(values_in[None], weight, (1, 1), 'VALID', dimens...]
    dot_general x4 -> x0, matrix products: 29.5 us -> none  [the longest x1 13.3 us: body(): jnp.einsum('hqk,hkd->hqd', weights, keys_vals[1], preferred_element_type=...]
    pallas_call x0 -> x3, Pallas kernels: none -> 27.3 us  [the longest x1 15.5 us: body(): pl.pallas_call(attention_kernel, out_shape=jax.ShapeDtypeStruct((HEADS *...]
    reduce_sum x5 -> x0, other arithmetic: 21.2 us -> none  [the longest x1 14.1 us: softmax_rows(): return raised / jnp.sum(raised, axis=-1, keepdims=True)]
    ppermute x11 -> x12, waiting for transfers between devices: 31.6 us -> 18.3 us  [the longest x3 10.5 us: body(): pieces.append(lax.ppermute(own, 'lon', pairs))]
    all_to_all x2, blocking collectives: 60.5 us -> 51.3 us  [the longest x1 27 us: body(): lax.all_to_all(outgoing, 'lon', 0, 0, axis_index_groups=groups, tiled=True)]
    squeeze x3 -> x0, local copies, waits for them, and re-layouts: 5.92 us -> none  [the longest x2 5.72 us: convolve(): lax.conv_general_dilated(values_in[None], weight, (1, 1), 'VALID', dimens...]
    ppermute x11 -> x12, starting transfers between devices: 36.9 us -> 32.2 us  [the longest x1 25.1 us: body(): high = lax.ppermute(field[:REACH], 'lon', backward)]
  transfers between devices with their start and end apart: 11 -> 12, of which waited for: 9 -> 6; matrix products, arithmetic and copies ran while one was open for 0% -> 0% of each run, Pallas kernels for 0% -> 0%
where the time goes in v1:
time: 139 us
  blocking collectives  51.3 us (37%)
  starting transfers between devices  32.2 us (23%)
  Pallas kernels  27.3 us (20%)
  waiting for transfers between devices  18.3 us (13%)
  local copies, waits for them, and re-layouts  9.31 us (7%)
    all_to_all x1, blocking collectives, body(): lax.all_to_all(outgoing, 'lon', 0, 0, axis_index_groups=groups, tiled=True)  27 us
    ppermute x1, starting transfers between devices, body(): high = lax.ppermute(field[:REACH], 'lon', backward)  25.1 us
    all_to_all x1, blocking collectives, body(): lax.all_to_all(attended.reshape(HEADS, half, 128), 'lon', 0, 0, axis_inde...  24.3 us
    pallas_call x1, Pallas kernels, body(): pl.pallas_call(attention_kernel, out_shape=jax.ShapeDtypeStruct((HEADS *...  15.5 us
    ppermute x3, waiting for transfers between devices, body(): pieces.append(lax.ppermute(own, 'lon', pairs))  10.5 us
    pallas_call x1, Pallas kernels, body(): pl.pallas_call(conv_kernel, out_shape=(jax.ShapeDtypeStruct((count, CB),...  9.47 us
    unnamed x11, local copies, waits for them, and re-layouts  7.71 us
    ppermute x1, waiting for transfers between devices, body(): lat_low = lax.ppermute(edge[cols - REACH:], ('lon', 'lat'), across(forward))  5.03 us
  transfers between devices with their start and end apart: 12, of which 6 were waited for; matrix products, arithmetic and copies ran while one was open for 0% of the time, Pallas kernels for 0%

profile of v1, /device:TPU:40, one launch (start us, length us, event | category | flops | bytes accessed | tf_op | source)
XLA Modules:
  0.0 138.6 jit_solution(10068118424215675126)
XLA Ops:
  0.0 1.1 copy.11
  1.2 0.1 collective-permute-start.2
  1.4 25.1 %collective-permute-start.1 = (bf16[3,128,256]{2,1,0:T(8,128)(2,1)S(1)}, bf16[3,128,256]{2,1,0:T(8,128)(2,1)S(1)}, u32[]{:S(2)}, u32[]{:S(2)}) collective-permute-start(bf16[3,128,256]{2,1,0:T(8,128)(2,1)S(1)} %get-tuple-element.9), channel_id=1, source_target_pairs={{2,0},{4,2},{6,4},{8,6},{10,8},{12,10},{14,12},{16,14},{18,16},{20... | collective-permute-start | bytes 589832 | tf_op jit(solution)/shard_map/ppermute | solution.py:216
  26.5 0.0 collective-permute-start
  26.5 4.9 %collective-permute-start.4 = (bf16[3,3,256]{2,1,0:T(4,128)(2,1)S(1)}, bf16[3,3,256]{2,1,0:T(4,128)(2,1)S(1)}, u32[]{:S(2)}, u32[]{:S(2)}) collective-permute-start(bf16[3,3,256]{2,1,0:T(4,128)(2,1)S(1)} %get-tuple-element.11), channel_id=1, source_target_pairs={{2,1},{3,0},{4,3},{5,2},{6,5},{7,4},{8,7},{9,6},{10,9},{11,8},{12,... | collective-permute-start | bytes 13832 | tf_op jit(solution)/shard_map/ppermute | solution.py:219
  31.3 0.0 collective-permute-start.3
  31.3 0.1 pad_add_fusion.lat_ref
  31.4 1.3 collective-permute-done.4.lat_high_ref
  32.7 5.0 %collective-permute-done.3.lat_low_ref = bf16[3,3,256]{2,1,0:T(4,128)(2,1)S(1)} collective-permute-done((bf16[3,3,256]{2,1,0:T(4,128)(2,1)S(1)}, bf16[3,3,256]{2,1,0:T(4,128)(2,1)S(1)}, u32[]{:S(2)}, u32[]{:S(2)}) %collective-permute-start.3) | collective-permute-done | bytes 4640 | tf_op jit(solution)/shard_map/ppermute | solution.py:218
  37.7 0.0 collective-permute-done.2.lat_mid_ref
  37.7 0.0 collective-permute-done.1.high_ref
  37.7 0.0 collective-permute-done.low_ref
  37.7 0.0 copy-start
  37.7 2.3 %copy-done = bf16[3,3,512,512]{3,2,1,0:T(8,128)(2,1)S(1)} copy-done((bf16[3,3,512,512]{3,2,1,0:T(8,128)(2,1)S(1)}, bf16[3,3,512,512]{3,2,1,0:T(8,128)(2,1)}, u32[]{:S(2)}) %copy-start) | copy-done | bytes 4718616
  40.1 0.0 copy-start.1
  40.1 1.9 %copy-done.1 = bf16[512,3072]{1,0:T(8,128)(2,1)S(1)} copy-done((bf16[512,3072]{1,0:T(8,128)(2,1)S(1)}, bf16[512,3072]{1,0:T(8,128)(2,1)}, u32[]{:S(2)}) %copy-start.1) | copy-done | bytes 3145752
  42.0 0.0 copy-start.2
  42.0 1.7 %copy-done.2 = bf16[3,3,256,512]{3,2,1,0:T(8,128)(2,1)S(1)} copy-done((bf16[3,3,256,512]{3,2,1,0:T(8,128)(2,1)S(1)}, bf16[3,3,256,512]{3,2,1,0:T(8,128)(2,1)}, u32[]{:S(2)}) %copy-start.2) | copy-done | bytes 2359320
  43.6 0.0 copy-start.4
  43.6 0.7 copy-done.4
  44.3 9.5 %convs.1 = (f32[64,512]{1,0:T(8,128)S(1)}, bf16[16,96,128]{2,1,0:T(8,128)(2,1)S(1)}) custom-call(s32[2]{0:T(128)S(1)} %pad_add_fusion.lat_ref, bf16[8,128,256]{2,1,0:T(8,128)(2,1)S(1)} %bitcast.17, bf16[3,128,256]{2,1,0:T(8,128)(2,1)S(1)} %collective-permute-done.low_ref, bf16[3,128,256]{2,1,0:T(8,128)(2,1)S(1)} %collective-permute-done.1.high_ref, ...), custom_call_target="tpu_custom_call" | custom-call | tf_op jit(solution)/shard_map/convs/pallas_call | solution.py:229
  53.8 0.0 copy-start.3
  53.8 27.0 %all_to_all.10 = bf16[16,96,128]{2,1,0:T(8,128)(2,1)S(1)} all-to-all(bf16[16,96,128]{2,1,0:T(8,128)(2,1)S(1)} %get-tuple-element.7), channel_id=1, replica_groups={{0,2,4,6,8,10,12,14,16,18,20,22,24,26,28,30},{32,34,36,38,40,42,44,46,4..., dimensions={0} | all-to-all | bytes 786432 | tf_op jit(solution)/shard_map/all_to_all | solution.py:257
  80.8 0.1 collective-permute-start.7
  81.0 0.3 collective-permute-start.6
  81.3 1.7 %collective-permute-start.5 = (bf16[1024,128]{1,0:T(8,128)(2,1)S(1)}, bf16[1024,128]{1,0:T(8,128)(2,1)S(1)}, u32[]{:S(2)}, u32[]{:S(2)}) collective-permute-start(bf16[1024,128]{1,0:T(8,128)(2,1)S(1)} %bitcast.21), channel_id=1, source_target_pairs={{0,32},{2,34},{4,36},{6,38},{8,40},{10,42},{12,44},{14,46},{16,48}... | collective-permute-start | bytes 786440 | tf_op jit(solution)/shard_map/ppermute | solution.py:267
  83.0 0.0 collective-permute-start.8
  83.0 5.9 %collective-permute-done.7.refs_3_ = bf16[1024,128]{1,0:T(8,128)(2,1)S(1)} collective-permute-done((bf16[1024,128]{1,0:T(8,128)(2,1)S(1)}, bf16[1024,128]{1,0:T(8,128)(2,1)S(1)}, u32[]{:S(2)}, u32[]{:S(2)}) %collective-permute-start.7) | collective-permute-done | bytes 262176 | tf_op jit(solution)/shard_map/ppermute | solution.py:267
  88.9 0.0 collective-permute-start.11
  88.9 1.9 %collective-permute-done.6.refs_2_ = bf16[1024,128]{1,0:T(8,128)(2,1)S(1)} collective-permute-done((bf16[1024,128]{1,0:T(8,128)(2,1)S(1)}, bf16[1024,128]{1,0:T(8,128)(2,1)S(1)}, u32[]{:S(2)}, u32[]{:S(2)}) %collective-permute-start.6) | collective-permute-done | bytes 262176 | tf_op jit(solution)/shard_map/ppermute | solution.py:267
  90.8 0.0 collective-permute-start.10
  90.8 2.7 %collective-permute-done.5.refs_1_ = bf16[1024,128]{1,0:T(8,128)(2,1)S(1)} collective-permute-done((bf16[1024,128]{1,0:T(8,128)(2,1)S(1)}, bf16[1024,128]{1,0:T(8,128)(2,1)S(1)}, u32[]{:S(2)}, u32[]{:S(2)}) %collective-permute-start.5) | collective-permute-done | bytes 262176 | tf_op jit(solution)/shard_map/ppermute | solution.py:267
  93.5 0.0 collective-permute-start.9
  93.5 0.0 collective-permute-done.8.refs_4_
  93.5 0.0 collective-permute-done.11.refs_7_
  93.5 0.0 collective-permute-done.10.refs_6_
  93.5 1.5 %collective-permute-done.9.refs_5_ = bf16[1024,128]{1,0:T(8,128)(2,1)S(1)} collective-permute-done((bf16[1024,128]{1,0:T(8,128)(2,1)S(1)}, bf16[1024,128]{1,0:T(8,128)(2,1)S(1)}, u32[]{:S(2)}, u32[]{:S(2)}) %collective-permute-start.9) | collective-permute-done | bytes 262176 | tf_op jit(solution)/shard_map/ppermute | solution.py:268
  95.0 15.5 %attention.1 = bf16[512,128]{1,0:T(8,128)(2,1)S(1)} custom-call(bf16[512,128]{1,0:T(8,128)(2,1)S(1)} %bitcast.24, bf16[1024,128]{1,0:T(8,128)(2,1)S(1)} %bitcast.23, bf16[1024,128]{1,0:T(8,128)(2,1)S(1)} %collective-permute-done.5.refs_1_, bf16[1024,128]{1,0:T(8,128)(2,1)S(1)} %collective-permute-done.6.refs_2_, ...), custom_call_target="tpu_custom_call" | custom-call | tf_op jit(solution)/shard_map/attention/pallas_call | solution.py:269
  110.5 24.3 %all_to_all.11.back_ref = bf16[16,32,128]{2,1,0:T(8,128)(2,1)} all-to-all(bf16[16,32,128]{2,1,0:T(8,128)(2,1)S(1)} %bitcast.25), channel_id=1, replica_groups={{0,2,4,6,8,10,12,14,16,18,20,22,24,26,28,30},{32,34,36,38,40,42,44,46,4..., dimensions={0} | all-to-all | bytes 262144 | tf_op jit(solution)/shard_map/all_to_all | solution.py:281
  134.8 0.0 copy-done.3
  134.8 2.3 %mix.1 = bf16[64,512]{1,0:T(8,128)(2,1)} custom-call(bf16[16,32,128]{2,1,0:T(8,128)(2,1)} %all_to_all.11.back_ref, f32[64,512]{1,0:T(8,128)} %copy-done.3, bf16[1024,512]{1,0:T(8,128)(2,1)} %weight_ref.1), custom_call_target="tpu_custom_call" | custom-call | tf_op jit(solution)/shard_map/mix/pallas_call | solution.py:284
  137.1 1.5 %copy.12 = bf16[2,32,512]{2,0,1:T(2,128)(2,1)} copy(bf16[2,32,512]{2,1,0:T(8,128)(2,1)} %bitcast.27) | data formatting | bytes 131072 | tf_op jit(solution)/shard_map/reshape | solution.py:291
  (5 shorter events, 0.1 us)
Async XLA Ops:
  1.2 36.5 %collective-permute-start.2 = (bf16[8,3,256]{2,1,0:T(4,128)(2,1)S(1)}, bf16[8,3,256]{2,1,0:T(4,128)(2,1)S(1)}, u32[]{:S(2)}, u32[]{:S(2)}) collective-permute-start(bf16[8,3,256]{2,1,0:T(4,128)(2,1)S(1)} %slice_select_fusion), channel_id=1, source_target_pairs={{0,1},{1,0},{2,3},{3,2},{4,5},{5,4},{6,7},{7,6},{8,9},{9,8},{10,11... | collective-permute-start | bytes 36872 | tf_op jit(solution)/shard_map/ppermute | solution.py:217
  1.4 36.4 %collective-permute-start.1 = (bf16[3,128,256]{2,1,0:T(8,128)(2,1)S(1)}, bf16[3,128,256]{2,1,0:T(8,128)(2,1)S(1)}, u32[]{:S(2)}, u32[]{:S(2)}) collective-permute-start(bf16[3,128,256]{2,1,0:T(8,128)(2,1)S(1)} %get-tuple-element.9), channel_id=1, source_target_pairs={{2,0},{4,2},{6,4},{8,6},{10,8},{12,10},{14,12},{16,14},{18,16},{20... | collective-permute-start | bytes 589832 | tf_op jit(solution)/shard_map/ppermute | solution.py:216
  26.5 11.3 %collective-permute-start = (bf16[3,128,256]{2,1,0:T(8,128)(2,1)S(1)}, bf16[3,128,256]{2,1,0:T(8,128)(2,1)S(1)}, u32[]{:S(2)}, u32[]{:S(2)}) collective-permute-start(bf16[3,128,256]{2,1,0:T(8,128)(2,1)S(1)} %get-tuple-element.10), channel_id=1, source_target_pairs={{0,2},{2,4},{4,6},{6,8},{8,10},{10,12},{12,14},{14,16},{16,18},{18... | collective-permute-start | bytes 589832 | tf_op jit(solution)/shard_map/ppermute | solution.py:215
  26.5 6.2 %collective-permute-start.4 = (bf16[3,3,256]{2,1,0:T(4,128)(2,1)S(1)}, bf16[3,3,256]{2,1,0:T(4,128)(2,1)S(1)}, u32[]{:S(2)}, u32[]{:S(2)}) collective-permute-start(bf16[3,3,256]{2,1,0:T(4,128)(2,1)S(1)} %get-tuple-element.11), channel_id=1, source_target_pairs={{2,1},{3,0},{4,3},{5,2},{6,5},{7,4},{8,7},{9,6},{10,9},{11,8},{12,... | collective-permute-start | bytes 13832 | tf_op jit(solution)/shard_map/ppermute | solution.py:219
  31.3 6.4 %collective-permute-start.3 = (bf16[3,3,256]{2,1,0:T(4,128)(2,1)S(1)}, bf16[3,3,256]{2,1,0:T(4,128)(2,1)S(1)}, u32[]{:S(2)}, u32[]{:S(2)}) collective-permute-start(bf16[3,3,256]{2,1,0:T(4,128)(2,1)S(1)} %get-tuple-element.12), channel_id=1, source_target_pairs={{0,3},{1,2},{2,5},{3,4},{4,7},{5,6},{6,9},{7,8},{8,11},{9,10},{10,... | collective-permute-start | bytes 13832 | tf_op jit(solution)/shard_map/ppermute | solution.py:218
  37.7 2.3 %copy-start = (bf16[3,3,512,512]{3,2,1,0:T(8,128)(2,1)S(1)}, bf16[3,3,512,512]{3,2,1,0:T(8,128)(2,1)}, u32[]{:S(2)}) copy-start(bf16[3,3,512,512]{3,2,1,0:T(8,128)(2,1)} %param.8) | copy-start | bytes 14155780
  40.1 1.9 %copy-start.1 = (bf16[512,3072]{1,0:T(8,128)(2,1)S(1)}, bf16[512,3072]{1,0:T(8,128)(2,1)}, u32[]{:S(2)}) copy-start(bf16[512,3072]{1,0:T(8,128)(2,1)} %qkv_hbm.1) | copy-start | bytes 9437188
  42.0 1.7 %copy-start.2 = (bf16[3,3,256,512]{3,2,1,0:T(8,128)(2,1)S(1)}, bf16[3,3,256,512]{3,2,1,0:T(8,128)(2,1)}, u32[]{:S(2)}) copy-start(bf16[3,3,256,512]{3,2,1,0:T(8,128)(2,1)} %param.7) | copy-start | bytes 7077892
  43.6 0.7 copy-start.4
  53.8 81.0 %copy-start.3 = (f32[64,512]{1,0:T(8,128)}, f32[64,512]{1,0:T(8,128)S(1)}, u32[]{:S(2)}) copy-start(f32[64,512]{1,0:T(8,128)S(1)} %get-tuple-element.8.tok_ref) | copy-start | bytes 393220
  80.8 8.0 %collective-permute-start.7 = (bf16[1024,128]{1,0:T(8,128)(2,1)S(1)}, bf16[1024,128]{1,0:T(8,128)(2,1)S(1)}, u32[]{:S(2)}, u32[]{:S(2)}) collective-permute-start(bf16[1024,128]{1,0:T(8,128)(2,1)S(1)} %bitcast.19), channel_id=1, source_target_pairs={{0,96},{2,98},{4,100},{6,102},{8,104},{10,106},{12,108},{14,110},{... | collective-permute-start | bytes 786440 | tf_op jit(solution)/shard_map/ppermute | solution.py:267
  81.0 9.8 %collective-permute-start.6 = (bf16[1024,128]{1,0:T(8,128)(2,1)S(1)}, bf16[1024,128]{1,0:T(8,128)(2,1)S(1)}, u32[]{:S(2)}, u32[]{:S(2)}) collective-permute-start(bf16[1024,128]{1,0:T(8,128)(2,1)S(1)} %bitcast.20), channel_id=1, source_target_pairs={{0,64},{2,66},{4,68},{6,70},{8,72},{10,74},{12,76},{14,78},{16,80}... | collective-permute-start | bytes 786440 | tf_op jit(solution)/shard_map/ppermute | solution.py:267
  81.3 12.1 %collective-permute-start.5 = (bf16[1024,128]{1,0:T(8,128)(2,1)S(1)}, bf16[1024,128]{1,0:T(8,128)(2,1)S(1)}, u32[]{:S(2)}, u32[]{:S(2)}) collective-permute-start(bf16[1024,128]{1,0:T(8,128)(2,1)S(1)} %bitcast.21), channel_id=1, source_target_pairs={{0,32},{2,34},{4,36},{6,38},{8,40},{10,42},{12,44},{14,46},{16,48}... | collective-permute-start | bytes 786440 | tf_op jit(solution)/shard_map/ppermute | solution.py:267
  83.0 10.5 %collective-permute-start.8 = (bf16[1024,128]{1,0:T(8,128)(2,1)S(1)}, bf16[1024,128]{1,0:T(8,128)(2,1)S(1)}, u32[]{:S(2)}, u32[]{:S(2)}) collective-permute-start(bf16[1024,128]{1,0:T(8,128)(2,1)S(1)} %bitcast.22), channel_id=1, source_target_pairs={{0,1},{1,0},{2,3},{3,2},{4,5},{5,4},{6,7},{7,6},{8,9},{9,8},{10,11... | collective-permute-start | bytes 786440 | tf_op jit(solution)/shard_map/ppermute | solution.py:268
  88.9 4.6 %collective-permute-start.11 = (bf16[1024,128]{1,0:T(8,128)(2,1)S(1)}, bf16[1024,128]{1,0:T(8,128)(2,1)S(1)}, u32[]{:S(2)}, u32[]{:S(2)}) collective-permute-start(bf16[1024,128]{1,0:T(8,128)(2,1)S(1)} %collective-permute-done.7.refs_3_), channel_id=1, source_target_pairs={{0,1},{1,0},{2,3},{3,2},{4,5},{5,4},{6,7},{7,6},{8,9},{9,8},{10,11... | collective-permute-start | bytes 786440 | tf_op jit(solution)/shard_map/ppermute | solution.py:268
  90.8 2.7 %collective-permute-start.10 = (bf16[1024,128]{1,0:T(8,128)(2,1)S(1)}, bf16[1024,128]{1,0:T(8,128)(2,1)S(1)}, u32[]{:S(2)}, u32[]{:S(2)}) collective-permute-start(bf16[1024,128]{1,0:T(8,128)(2,1)S(1)} %collective-permute-done.6.refs_2_), channel_id=1, source_target_pairs={{0,1},{1,0},{2,3},{3,2},{4,5},{5,4},{6,7},{7,6},{8,9},{9,8},{10,11... | collective-permute-start | bytes 786440 | tf_op jit(solution)/shard_map/ppermute | solution.py:268
  93.5 1.5 %collective-permute-start.9 = (bf16[1024,128]{1,0:T(8,128)(2,1)S(1)}, bf16[1024,128]{1,0:T(8,128)(2,1)S(1)}, u32[]{:S(2)}, u32[]{:S(2)}) collective-permute-start(bf16[1024,128]{1,0:T(8,128)(2,1)S(1)} %collective-permute-done.5.refs_1_), channel_id=1, source_target_pairs={{0,1},{1,0},{2,3},{3,2},{4,5},{5,4},{6,7},{7,6},{8,9},{9,8},{10,11... | collective-permute-start | bytes 786440 | tf_op jit(solution)/shard_map/ppermute | solution.py:268

commit v2 on v1

--- a/solution.py
+++ b/solution.py
@@ -12,6 +12,7 @@
 HEADS = 16
 HEAD_DIM = 64
 REACH = 3
+PIECES = 2
 BF = jnp.bfloat16
 F32 = jnp.float32
 VMEM = pl.BlockSpec(memory_space=pltpu.VMEM)
@@ -29,7 +30,7 @@
 
 
 def conv_kernel(
-    lat_ref, mid_ref, low_ref, high_ref, lat_mid_ref, lat_low_ref, lat_high_ref, gain_ref,
+    lat_ref, mid_ref, low_ref, high_ref, edge_ref, gain_ref,
     conv_a_hbm, conv_b_hbm, qkv_hbm,
     tok_ref, out_ref,
     conv_a_ref, conv_b_ref, qkv_ref, wide, shifted, pool_a, ready, pool_b, sems,
@@ -45,14 +46,14 @@
     last = lat_ref[1] - 1
     cols, rows, chans = mid_ref.shape
     span = shifted.shape[2]
-    for ref, edge, at in (
-        (low_ref, lat_low_ref, 0),
-        (mid_ref, lat_mid_ref, REACH),
-        (high_ref, lat_high_ref, REACH + cols),
+    for ref, edge_rows, at in (
+        (low_ref, low_ref[:, rows:], 0),
+        (mid_ref, edge_ref[...], REACH),
+        (high_ref, high_ref[:, rows:], REACH + cols),
     ):
         n = ref.shape[0]
-        wide[at : at + n, REACH : REACH + rows, :] = ref[...].astype(F32)
-        rows_edge = edge[...].astype(F32)
+        wide[at : at + n, REACH : REACH + rows, :] = ref[:, :rows].astype(F32)
+        rows_edge = edge_rows.astype(F32)
         nothing = jnp.zeros_like(rows_edge)
         wide[at : at + n, 0:REACH, :] = jnp.where(lat == 0, nothing, rows_edge)
         wide[at : at + n, REACH + rows : 2 * REACH + rows, :] = jnp.where(
@@ -138,44 +139,95 @@
         out_ref[h + 1, count:] = jnp.where(below_half, turned[0][:half], q[half:]).astype(BF)
 
 
-def attention_kernel(q_ref, *refs):
-    kv_refs, (out_ref, queries, ones_vals) = refs[:-3], refs[-3:]
-    packed_rows = q_ref.shape[0]
+def attention_kernel(first, final, *refs):
+    refs = list(refs)
+    q_ref = refs.pop(0)
+    kv_refs = [refs.pop(0) for _ in range(PIECES)]
+    held = None if first else (refs.pop(0), refs.pop(0))
+    ones_vals = refs.pop()
+    queries, acc_ref, top_ref = (None, None, None) if final else refs if first else (None, *refs)
     keys = kv_refs[0].shape[0]
-    packed = q_ref[...].astype(F32)
-    below = lanes_of((packed_rows, 128)) < HEAD_DIM
-    zero = jnp.zeros_like(packed)
-    queries[0] = jnp.where(below, packed, zero).astype(BF)
-    queries[1] = jnp.where(below, pltpu.roll(packed, HEAD_DIM, 1), zero).astype(BF)
+    mask_keys = lanes_of((keys, 128)) < HEAD_DIM
+    if first:
+        rows = q_ref.shape[0]
+        packed = q_ref[...].astype(F32)
+        below = lanes_of((rows, 128)) < HEAD_DIM
+        zero = jnp.zeros_like(packed)
+        queries[0] = jnp.where(below, packed, zero).astype(BF)
+        queries[1] = jnp.where(below, pltpu.roll(packed, HEAD_DIM, 1), zero).astype(BF)
+    else:
+        queries = q_ref
+        rows = q_ref.shape[1]
     one = jnp.ones((keys, 128), BF)
-    below_keys = lanes_of((keys, 128)) < HEAD_DIM
     for i, kv in enumerate(kv_refs):
-        ones_vals[i] = jnp.where(below_keys, one, kv[...])
+        ones_vals[i] = jnp.where(mask_keys, one, kv[...])
     factor = HEAD_DIM ** (-0.5) * math.log2(math.e)
-    block = 128
-
-    def step(j, carry):
-        at = pl.multiple_of(j * block, block)
-        q = queries[:, pl.ds(at, block), :].reshape(2 * block, 128)
-        top = jnp.full((2 * block, 1), -jnp.inf, F32)
-        acc = jnp.zeros((2 * block, 128), F32)
-        for i, kv in enumerate(kv_refs):
-            scores = lax.dot_general(
-                q, kv[...], (((1,), (1,)), ((), ())), preferred_element_type=F32
-            )
-            new_top = jnp.maximum(top, jnp.max(scores, axis=-1, keepdims=True))
-            raised = jnp.exp2((scores - new_top) * factor).astype(BF)
-            part = jnp.dot(raised, ones_vals[i], preferred_element_type=F32)
-            acc = part if i == 0 else acc * jnp.exp2((top - new_top) * factor) + part
-            top = new_top
+    block = rows // 2
+    units = [(at, i) for at in range(0, rows, block) for i in range(PIECES)]
+
+    def score(unit):
+        at, i = unit
+        return lax.dot_general(
+            queries[:, at : at + block, :].reshape(2 * block, 128),
+            kv_refs[i][...],
+            (((1,), (1,)), ((), ())),
+            preferred_element_type=F32,
+        )
+
+    ahead = score(units[0])
+    for n, (at, i) in enumerate(units):
+        scores = ahead
+        if n + 1 < len(units):
+            ahead = score(units[n + 1])
+        if i == 0:
+            if first:
+                top = jnp.full((2 * block, 1), -jnp.inf, F32)
+                acc = None
+            else:
+                top = held[1][:, at : at + block, :].reshape(2 * block, 128)[:, :1]
+                acc = held[0][:, at : at + block, :].reshape(2 * block, 128)
+        new_top = jnp.maximum(top, jnp.max(scores, axis=-1, keepdims=True))
+        raised = jnp.exp2((scores - new_top) * factor).astype(BF)
+        part = jnp.dot(raised, ones_vals[i], preferred_element_type=F32)
+        acc = part if acc is None else acc * jnp.exp2((top - new_top) * factor) + part
+        top = new_top
+        if i < PIECES - 1:
+            continue
+        if not final:
+            acc_ref[:, at : at + block, :] = acc.reshape(2, block, 128)
+            wide = jnp.broadcast_to(top, (2 * block, 128))
+            top_ref[:, at : at + block, :] = wide.reshape(2, block, 128)
+            continue
         turned = pltpu.roll(acc, HEAD_DIM, 1)
         low = turned[:block] / acc[:block]
         high = acc[block:] / turned[block:]
         mask = lanes_of((block, 128)) < HEAD_DIM
-        out_ref[pl.ds(at, block), :] = jnp.where(mask, low, high).astype(BF)
-        return carry
-
-    lax.fori_loop(0, packed_rows // block, step, 0)
+        refs[0][at : at + block, :] = jnp.where(mask, low, high).astype(BF)
+
+
+def attend(queries, pieces, held, final):
+    first = held is None
+    rows = queries.shape[0] if first else queries.shape[1]
+    keys = pieces[0].shape[0]
+    state = [jax.ShapeDtypeStruct((2, rows, 128), F32)] * 2
+    if final:
+        outs = jax.ShapeDtypeStruct((rows, 128), BF)
+    else:
+        outs = tuple(([jax.ShapeDtypeStruct((2, rows, 128), BF)] if first else []) + state)
+    return pl.pallas_call(
+        functools.partial(attention_kernel, first, final),
+        out_shape=outs,
+        in_specs=[VMEM] * (1 + PIECES + (0 if first else 2)),
+        out_specs=VMEM if final else (VMEM,) * len(outs),
+        scratch_shapes=[pltpu.VMEM((PIECES, keys, 128), BF)],
+        compiler_params=pltpu.CompilerParams(vmem_limit_bytes=24 * 2**20),
+        cost_estimate=pl.CostEstimate(
+            flops=4 * 2 * rows * PIECES * keys * 256,
+            transcendentals=2 * rows * PIECES * keys,
+            bytes_accessed=2**22,
+        ),
+        name="attention",
+    )(queries, *pieces, *(held or ()))
 
 
 def out_kernel(back_ref, tok_ref, weight_ref, out_ref):
@@ -191,7 +243,10 @@
         [jnp.concatenate(low, axis=1), jnp.concatenate(high, axis=1)], axis=0
     )
     mixed = tok_ref[...] + jnp.dot(attended, weight_ref[...], preferred_element_type=F32)
-    out_ref[...] = mixed.astype(BF)
+    cols = out_ref.shape[1]
+    rows = out_ref.shape[0]
+    columns = [mixed[c * rows : (c + 1) * rows] for c in range(cols)]
+    out_ref[...] = jnp.stack(columns, axis=1).astype(BF)
 
 
 def body(surface_field, conv_a, conv_b, norm_gain, qkv_weight, out_weight):
@@ -199,24 +254,22 @@
     lat_count = lax.axis_size("lat")
     lat = lax.axis_index("lat")
     rows, cols, chans = surface_field.shape
-    field = surface_field.transpose(1, 0, 2)
     forward = [(i, (i + 1) % lon_count) for i in range(lon_count)]
     backward = [(target, source) for source, target in forward]
-
-    def across(pairs):
-        return [
-            (s * lat_count + c, t * lat_count + (c + 1) % lat_count)
-            for s, t in pairs
-            for c in range(lat_count)
-        ]
-
     swap = [(c, (c + 1) % lat_count) for c in range(lat_count)]
-    edge = jnp.where(lat == 0, field[:, rows - REACH :], field[:, :REACH])
-    low = lax.ppermute(field[cols - REACH :], "lon", forward)
-    high = lax.ppermute(field[:REACH], "lon", backward)
-    lat_mid = lax.ppermute(edge, "lat", swap)
-    lat_low = lax.ppermute(edge[cols - REACH :], ("lon", "lat"), across(forward))
-    lat_high = lax.ppermute(edge[:REACH], ("lon", "lat"), across(backward))
+    first_row = jnp.where(lat == 0, rows - REACH, 0)
+    edge = lax.ppermute(
+        lax.dynamic_slice_in_dim(surface_field, first_row, REACH, axis=0), "lat", swap
+    )
+
+    def columns(at):
+        beyond = jnp.concatenate([surface_field[:, at : at + REACH], edge[:, at : at + REACH]])
+        return beyond.transpose(1, 0, 2)
+
+    low = lax.ppermute(columns(cols - REACH), "lon", forward)
+    high = lax.ppermute(columns(0), "lon", backward)
+    field = surface_field.transpose(1, 0, 2)
+    edge = edge.transpose(1, 0, 2)
 
     wide_cols = cols + 2 * REACH
     span = -(-(rows + 4) // 16) * 16
@@ -232,7 +285,7 @@
             jax.ShapeDtypeStruct((count, CB), F32),
             jax.ShapeDtypeStruct((HEADS, count + half, 128), BF),
         ),
-        in_specs=[SMEM] + [VMEM] * 7 + [HBM] * 3,
+        in_specs=[SMEM] + [VMEM] * 5 + [HBM] * 3,
         out_specs=(VMEM, VMEM),
         scratch_shapes=[
             pltpu.VMEM((9 * chans, CB), BF),
@@ -248,8 +301,8 @@
         compiler_params=pltpu.CompilerParams(vmem_limit_bytes=40 * 2**20),
         name="convs",
     )(
-        where, field, low, high, lat_mid, lat_low, lat_high, norm_gain.reshape(1, CB),
-        conv_a.reshape(9 * chans, CB), conv_b.reshape(9 * CB, CB), qkv_weight,
+        where, field, low, high, edge, norm_gain.reshape(1, CB),
+        *[pltpu.with_memory_space_constraint(w, pltpu.HBM) for w in (conv_a.reshape(9 * chans, CB), conv_b.reshape(9 * CB, CB), qkv_weight)],
     )
 
     residues = lon_count // HEADS
@@ -257,38 +310,41 @@
     arrived = lax.all_to_all(outgoing, "lon", 0, 0, axis_index_groups=groups, tiled=True)
     queries = arrived[:, count:].reshape(HEADS * half, 128)
     own = arrived[:, :count].reshape(HEADS * count, 128)
-    pieces = [own]
-    for d in range(1, residues):
+
+    def beside(value, d):
         pairs = [
             (r * HEADS + h, (r + d) % residues * HEADS + h)
             for r in range(residues)
             for h in range(HEADS)
         ]
-        pieces.append(lax.ppermute(own, "lon", pairs))
-    pieces += [lax.ppermute(piece, "lat", swap) for piece in pieces]
-    attended = pl.pallas_call(
-        attention_kernel,
-        out_shape=jax.ShapeDtypeStruct((HEADS * half, 128), BF),
-        in_specs=[VMEM] * (1 + len(pieces)),
-        out_specs=VMEM,
-        scratch_shapes=[
-            pltpu.VMEM((2, HEADS * half, 128), BF),
-            pltpu.VMEM((len(pieces), HEADS * count, 128), BF),
-        ],
-        compiler_params=pltpu.CompilerParams(vmem_limit_bytes=40 * 2**20),
-        name="attention",
-    )(queries, *pieces)
+        return lax.ppermute(value, "lon", pairs)
+
+    def other(value):
+        return lax.ppermute(value, "lat", swap)
+
+    near = beside(own, 1)
+    near_back = beside(own, residues - 1)
+    far = beside(own, 2)
+    own_other = other(own)
+    queries, *held = attend(queries, [own, own_other], None, False)
+    near_other = other(near)
+    near_back_other = other(near_back)
+    held = attend(queries, [near, near_back], held, False)
+    far_other = other(far)
+    held = attend(queries, [near_other, near_back_other], held, False)
+    attended = attend(queries, [far, far_other], held, True)
     returned = lax.all_to_all(
         attended.reshape(HEADS, half, 128), "lon", 0, 0, axis_index_groups=groups, tiled=True
     )
     mixed = pl.pallas_call(
         out_kernel,
-        out_shape=jax.ShapeDtypeStruct((count, CB), BF),
+        out_shape=jax.ShapeDtypeStruct((rows // 4, cols // 4, CB), BF),
         in_specs=[VMEM] * 3,
         out_specs=VMEM,
+        compiler_params=pltpu.CompilerParams(vmem_limit_bytes=16 * 2**20),
         name="mix",
     )(returned, tokens, out_weight)
-    return mixed.reshape(cols // 4, rows // 4, CB).transpose(1, 0, 2)
+    return mixed
 
 
 def solution(mesh):

time: 139 us -> 124 us (0.89)
  local copies, waits for them, and re-layouts: 9.31 us -> 1.91 us
  Pallas kernels: 27.3 us -> 22.8 us
  starting transfers between devices: 32.2 us -> 29.5 us
  blocking collectives: 51.3 us -> 49.2 us
  waiting for transfers between devices: 18.3 us -> 19.9 us
    unnamed x11 -> x5, local copies, waits for them, and re-layouts: 7.71 us -> 1.83 us
    pallas_call x2 -> x5, Pallas kernels: 17.8 us -> 13.3 us  [the longest x4 12.2 us: attend(): pl.pallas_call(functools.partial(attention_kernel, first, final), out_sha...]
    ppermute x12 -> x10, starting transfers between devices: 32.2 us -> 29.5 us  [the longest x1 25.1 us: body(): high = lax.ppermute(columns(0), 'lon', backward)]
    ppermute x12 -> x10, waiting for transfers between devices: 18.3 us -> 19.9 us  [the longest x3 8.63 us: beside(): return lax.ppermute(value, 'lon', pairs)]
    all_to_all x1, blocking collectives: 27 us -> 25.4 us  [body(): lax.all_to_all(outgoing, 'lon', 0, 0, axis_index_groups=groups, tiled=True)]
    reshape x1 -> x0, local copies, waits for them, and re-layouts: 1.54 us -> none  [body(): return mixed.reshape(cols // 4, rows // 4, CB).transpose(1, 0, 2)]
  transfers between devices with their start and end apart: 12 -> 10, of which waited for: 6 -> 4; matrix products, arithmetic and copies ran while one was open for 0% -> 0% of each run, Pallas kernels for 0% -> 7%
where the time goes in v2:
time: 124 us
  blocking collectives  49.2 us (40%)
  starting transfers between devices  29.5 us (24%)
  Pallas kernels  22.8 us (18%)
  waiting for transfers between devices  19.9 us (16%)
  local copies, waits for them, and re-layouts  1.91 us (2%)
    all_to_all x1, blocking collectives, body(): lax.all_to_all(outgoing, 'lon', 0, 0, axis_index_groups=groups, tiled=True)  25.4 us
    ppermute x1, starting transfers between devices, body(): high = lax.ppermute(columns(0), 'lon', backward)  25.1 us
    all_to_all x1, blocking collectives, body(): lax.all_to_all(attended.reshape(HEADS, half, 128), 'lon', 0, 0, axis_inde...  23.8 us
    pallas_call x4, Pallas kernels, attend(): pl.pallas_call(functools.partial(attention_kernel, first, final), out_sha...  12.2 us
    pallas_call x1, Pallas kernels, body(): pl.pallas_call(conv_kernel, out_shape=(jax.ShapeDtypeStruct((count, CB),...  9.55 us
    ppermute x3, waiting for transfers between devices, beside(): return lax.ppermute(value, 'lon', pairs)  8.63 us
    ppermute x1, waiting for transfers between devices, body(): low = lax.ppermute(columns(cols - REACH), 'lon', forward)  5.65 us
    ppermute x1, waiting for transfers between devices, body(): high = lax.ppermute(columns(0), 'lon', backward)  4.51 us
  transfers between devices with their start and end apart: 10, of which 4 were waited for; matrix products, arithmetic and copies ran while one was open for 0% of the time, Pallas kernels for 7%

profile of v2, /device:TPU:40, one launch (start us, length us, event | category | flops | bytes accessed | tf_op | source)
XLA Modules:
  0.0 123.6 jit_solution(15777187818829843362)
XLA Ops:
  0.0 1.1 copy.13
  1.2 0.1 collective-permute-start
  1.4 1.1 collective-permute-done
  2.5 25.1 %collective-permute-start.2 = (bf16[3,131,256]{2,1,0:T(8,128)(2,1)S(1)}, bf16[3,131,256]{2,1,0:T(8,128)(2,1)S(1)}, u32[]{:S(2)}, u32[]{:S(2)}) collective-permute-start(bf16[3,131,256]{2,1,0:T(8,128)(2,1)S(1)} %maximum_bitcast_fusion.1), channel_id=1, source_target_pairs={{2,0},{4,2},{6,4},{8,6},{10,8},{12,10},{14,12},{16,14},{18,16},{20... | collective-permute-start | bytes 603656 | tf_op jit(solution)/shard_map/ppermute | solution.py:270
  27.6 0.1 collective-permute-start.1
  27.8 0.1 pad_add_fusion.lat_ref
  27.9 4.5 %collective-permute-done.2.high_ref = bf16[3,131,256]{2,1,0:T(8,128)(2,1)S(1)} collective-permute-done((bf16[3,131,256]{2,1,0:T(8,128)(2,1)S(1)}, bf16[3,131,256]{2,1,0:T(8,128)(2,1)S(1)}, u32[]{:S(2)}, u32[]{:S(2)}) %collective-permute-start.2) | collective-permute-done | bytes 201248 | tf_op jit(solution)/shard_map/ppermute | solution.py:270
  32.4 5.7 %collective-permute-done.1.low_ref = bf16[3,131,256]{2,1,0:T(8,128)(2,1)S(1)} collective-permute-done((bf16[3,131,256]{2,1,0:T(8,128)(2,1)S(1)}, bf16[3,131,256]{2,1,0:T(8,128)(2,1)S(1)}, u32[]{:S(2)}, u32[]{:S(2)}) %collective-permute-start.1) | collective-permute-done | bytes 201248 | tf_op jit(solution)/shard_map/ppermute | solution.py:269
  38.0 0.0 copy-start.1
  38.0 0.7 copy-done.1
  38.7 9.6 %convs.1 = (f32[64,512]{1,0:T(8,128)S(1)}, bf16[16,96,128]{2,1,0:T(8,128)(2,1)S(1)}) custom-call(s32[2]{0:T(128)S(1)} %pad_add_fusion.lat_ref, bf16[8,128,256]{2,1,0:T(8,128)(2,1)S(1)} %bitcast.14, bf16[3,131,256]{2,1,0:T(8,128)(2,1)S(1)} %collective-permute-done.1.low_ref, bf16[3,131,256]{2,1,0:T(8,128)(2,1)S(1)} %collective-permute-done.2.high_ref, ...), custom_call_target="tpu_custom_call" | custom-call | tf_op jit(solution)/shard_map/convs/pallas_call | solution.py:282
  48.3 25.4 %all_to_all.10 = bf16[16,96,128]{2,1,0:T(8,128)(2,1)S(1)} all-to-all(bf16[16,96,128]{2,1,0:T(8,128)(2,1)S(1)} %get-tuple-element.14), channel_id=1, replica_groups={{0,2,4,6,8,10,12,14,16,18,20,22,24,26,28,30},{32,34,36,38,40,42,44,46,4..., dimensions={0} | all-to-all | bytes 786432 | tf_op jit(solution)/shard_map/all_to_all | solution.py:310
  73.7 0.1 collective-permute-start.6
  73.9 3.2 %collective-permute-start.8 = (bf16[1024,128]{1,0:T(8,128)(2,1)S(1)}, bf16[1024,128]{1,0:T(8,128)(2,1)S(1)}, u32[]{:S(2)}, u32[]{:S(2)}) collective-permute-start(bf16[1024,128]{1,0:T(8,128)(2,1)S(1)} %bitcast.16), channel_id=1, source_target_pairs={{0,96},{2,98},{4,100},{6,102},{8,104},{10,106},{12,108},{14,110},{... | collective-permute-start | bytes 786440 | tf_op jit(solution)/shard_map/ppermute | solution.py:320
  77.1 0.0 collective-permute-start.4
  77.1 0.0 collective-permute-start.3
  77.1 8.6 %collective-permute-done.6.refs_1_ = bf16[1024,128]{1,0:T(8,128)(2,1)S(1)} collective-permute-done((bf16[1024,128]{1,0:T(8,128)(2,1)S(1)}, bf16[1024,128]{1,0:T(8,128)(2,1)S(1)}, u32[]{:S(2)}, u32[]{:S(2)}) %collective-permute-start.6) | collective-permute-done | bytes 262176 | tf_op jit(solution)/shard_map/ppermute | solution.py:320
  85.7 0.0 collective-permute-start.7
  85.7 0.0 collective-permute-done.8.refs_2_
  85.7 0.5 collective-permute-start.9
  86.2 0.0 collective-permute-done.4.refs_1_
  86.2 0.3 collective-permute-start.5
  86.6 0.0 collective-permute-done.3.refs_2_
  86.6 2.7 %attention.4 = (bf16[2,512,128]{2,1,0:T(8,128)(2,1)S(1)}, f32[2,512,128]{2,1,0:T(8,128)S(1)}, f32[2,512,128]{2,1,0:T(8,128)S(1)}) custom-call(bf16[512,128]{1,0:T(8,128)(2,1)S(1)} %bitcast.20, bf16[1024,128]{1,0:T(8,128)(2,1)S(1)} %bitcast.19, bf16[1024,128]{1,0:T(8,128)(2,1)S(1)} %collective-permute-done.3.refs_2_), custom_call_target="tpu_custom_call" | custom-call | flops 2147483648 | bytes 4194304 | tf_op jit(solution)/shard_map/attention/pallas_call | solution.py:217
  89.3 3.1 %attention.5 = (f32[2,512,128]{2,1,0:T(8,128)S(1)}, f32[2,512,128]{2,1,0:T(8,128)S(1)}) custom-call(bf16[2,512,128]{2,1,0:T(8,128)(2,1)S(1)} %get-tuple-element.15.refs_0_, bf16[1024,128]{1,0:T(8,128)(2,1)S(1)} %collective-permute-done.6.refs_1_, bf16[1024,128]{1,0:T(8,128)(2,1)S(1)} %collective-permute-done.8.refs_2_, ...), custom_call_target="tpu_custom_call" | custom-call | flops 2147483648 | bytes 4194304 | tf_op jit(solution)/shard_map/attention/pallas_call | solution.py:217
  92.4 0.0 collective-permute-done.7.refs_1_
  92.4 0.0 collective-permute-done.9.refs_2_
  92.4 3.1 %attention.6 = (f32[2,512,128]{2,1,0:T(8,128)S(1)}, f32[2,512,128]{2,1,0:T(8,128)S(1)}) custom-call(bf16[2,512,128]{2,1,0:T(8,128)(2,1)S(1)} %get-tuple-element.15.refs_0_, bf16[1024,128]{1,0:T(8,128)(2,1)S(1)} %collective-permute-done.7.refs_1_, bf16[1024,128]{1,0:T(8,128)(2,1)S(1)} %collective-permute-done.9.refs_2_, ...), custom_call_target="tpu_custom_call" | custom-call | flops 2147483648 | bytes 4194304 | tf_op jit(solution)/shard_map/attention/pallas_call | solution.py:217
  95.5 0.0 collective-permute-done.5.refs_2_
  95.5 0.0 copy-start
  95.5 3.3 %attention.7 = bf16[512,128]{1,0:T(8,128)(2,1)S(1)} custom-call(bf16[2,512,128]{2,1,0:T(8,128)(2,1)S(1)} %get-tuple-element.15.refs_0_, bf16[1024,128]{1,0:T(8,128)(2,1)S(1)} %collective-permute-done.4.refs_1_, bf16[1024,128]{1,0:T(8,128)(2,1)S(1)} %collective-permute-done.5.refs_2_, f32[2,512,128]{2,1,0:T(8,128)S(1)} %get-tuple-element.20.refs_3_, ...), custom_call_target="tpu_custom_call" | custom-call | flops 2147483648 | bytes 4194304 | tf_op jit(solution)/shard_map/attention/pallas_call | solution.py:217
  98.8 23.8 %all_to_all.11.back_ref = bf16[16,32,128]{2,1,0:T(8,128)(2,1)S(1)} all-to-all(bf16[16,32,128]{2,1,0:T(8,128)(2,1)S(1)} %bitcast.21), channel_id=1, replica_groups={{0,2,4,6,8,10,12,14,16,18,20,22,24,26,28,30},{32,34,36,38,40,42,44,46,4..., dimensions={0} | all-to-all | bytes 262144 | tf_op jit(solution)/shard_map/all_to_all | solution.py:336
  122.6 0.0 copy-done
  122.6 1.1 mix.1
  (7 shorter events, 0.1 us)
Async XLA Ops:
  1.2 1.3 %collective-permute-start = (bf16[3,8,256]{2,0,1:T(4,128)(2,1)S(1)}, bf16[3,8,256]{2,0,1:T(4,128)(2,1)S(1)}, u32[]{:S(2)}, u32[]{:S(2)}) collective-permute-start(bf16[3,8,256]{2,0,1:T(4,128)(2,1)S(1)} %constant_dynamic-slice_fusion), channel_id=1, source_target_pairs={{0,1},{1,0},{2,3},{3,2},{4,5},{5,4},{6,7},{7,6},{8,9},{9,8},{10,11... | collective-permute-start | bytes 36872 | tf_op jit(solution)/shard_map/ppermute | solution.py:261
  2.5 29.8 %collective-permute-start.2 = (bf16[3,131,256]{2,1,0:T(8,128)(2,1)S(1)}, bf16[3,131,256]{2,1,0:T(8,128)(2,1)S(1)}, u32[]{:S(2)}, u32[]{:S(2)}) collective-permute-start(bf16[3,131,256]{2,1,0:T(8,128)(2,1)S(1)} %maximum_bitcast_fusion.1), channel_id=1, source_target_pairs={{2,0},{4,2},{6,4},{8,6},{10,8},{12,10},{14,12},{16,14},{18,16},{20... | collective-permute-start | bytes 603656 | tf_op jit(solution)/shard_map/ppermute | solution.py:270
  27.6 10.4 %collective-permute-start.1 = (bf16[3,131,256]{2,1,0:T(8,128)(2,1)S(1)}, bf16[3,131,256]{2,1,0:T(8,128)(2,1)S(1)}, u32[]{:S(2)}, u32[]{:S(2)}) collective-permute-start(bf16[3,131,256]{2,1,0:T(8,128)(2,1)S(1)} %maximum_bitcast_fusion), channel_id=1, source_target_pairs={{0,2},{2,4},{4,6},{6,8},{8,10},{10,12},{12,14},{14,16},{16,18},{18... | collective-permute-start | bytes 603656 | tf_op jit(solution)/shard_map/ppermute | solution.py:269
  38.0 0.7 copy-start.1
  73.7 12.0 %collective-permute-start.6 = (bf16[1024,128]{1,0:T(8,128)(2,1)S(1)}, bf16[1024,128]{1,0:T(8,128)(2,1)S(1)}, u32[]{:S(2)}, u32[]{:S(2)}) collective-permute-start(bf16[1024,128]{1,0:T(8,128)(2,1)S(1)} %bitcast.15), channel_id=1, source_target_pairs={{0,32},{2,34},{4,36},{6,38},{8,40},{10,42},{12,44},{14,46},{16,48}... | collective-permute-start | bytes 786440 | tf_op jit(solution)/shard_map/ppermute | solution.py:320
  73.9 11.9 %collective-permute-start.8 = (bf16[1024,128]{1,0:T(8,128)(2,1)S(1)}, bf16[1024,128]{1,0:T(8,128)(2,1)S(1)}, u32[]{:S(2)}, u32[]{:S(2)}) collective-permute-start(bf16[1024,128]{1,0:T(8,128)(2,1)S(1)} %bitcast.16), channel_id=1, source_target_pairs={{0,96},{2,98},{4,100},{6,102},{8,104},{10,106},{12,108},{14,110},{... | collective-permute-start | bytes 786440 | tf_op jit(solution)/shard_map/ppermute | solution.py:320
  77.1 9.2 %collective-permute-start.4 = (bf16[1024,128]{1,0:T(8,128)(2,1)S(1)}, bf16[1024,128]{1,0:T(8,128)(2,1)S(1)}, u32[]{:S(2)}, u32[]{:S(2)}) collective-permute-start(bf16[1024,128]{1,0:T(8,128)(2,1)S(1)} %bitcast.17), channel_id=1, source_target_pairs={{0,64},{2,66},{4,68},{6,70},{8,72},{10,74},{12,76},{14,78},{16,80}... | collective-permute-start | bytes 786440 | tf_op jit(solution)/shard_map/ppermute | solution.py:320
  77.1 9.5 %collective-permute-start.3 = (bf16[1024,128]{1,0:T(8,128)(2,1)S(1)}, bf16[1024,128]{1,0:T(8,128)(2,1)S(1)}, u32[]{:S(2)}, u32[]{:S(2)}) collective-permute-start(bf16[1024,128]{1,0:T(8,128)(2,1)S(1)} %bitcast.18), channel_id=1, source_target_pairs={{0,1},{1,0},{2,3},{3,2},{4,5},{5,4},{6,7},{7,6},{8,9},{9,8},{10,11... | collective-permute-start | bytes 786440 | tf_op jit(solution)/shard_map/ppermute | solution.py:323
  85.7 6.7 %collective-permute-start.7 = (bf16[1024,128]{1,0:T(8,128)(2,1)S(1)}, bf16[1024,128]{1,0:T(8,128)(2,1)S(1)}, u32[]{:S(2)}, u32[]{:S(2)}) collective-permute-start(bf16[1024,128]{1,0:T(8,128)(2,1)S(1)} %collective-permute-done.6.refs_1_), channel_id=1, source_target_pairs={{0,1},{1,0},{2,3},{3,2},{4,5},{5,4},{6,7},{7,6},{8,9},{9,8},{10,11... | collective-permute-start | bytes 786440 | tf_op jit(solution)/shard_map/ppermute | solution.py:323
  85.7 6.7 %collective-permute-start.9 = (bf16[1024,128]{1,0:T(8,128)(2,1)S(1)}, bf16[1024,128]{1,0:T(8,128)(2,1)S(1)}, u32[]{:S(2)}, u32[]{:S(2)}) collective-permute-start(bf16[1024,128]{1,0:T(8,128)(2,1)S(1)} %collective-permute-done.8.refs_2_), channel_id=1, source_target_pairs={{0,1},{1,0},{2,3},{3,2},{4,5},{5,4},{6,7},{7,6},{8,9},{9,8},{10,11... | collective-permute-start | bytes 786440 | tf_op jit(solution)/shard_map/ppermute | solution.py:323
  86.2 9.3 %collective-permute-start.5 = (bf16[1024,128]{1,0:T(8,128)(2,1)S(1)}, bf16[1024,128]{1,0:T(8,128)(2,1)S(1)}, u32[]{:S(2)}, u32[]{:S(2)}) collective-permute-start(bf16[1024,128]{1,0:T(8,128)(2,1)S(1)} %collective-permute-done.4.refs_1_), channel_id=1, source_target_pairs={{0,1},{1,0},{2,3},{3,2},{4,5},{5,4},{6,7},{7,6},{8,9},{9,8},{10,11... | collective-permute-start | bytes 786440 | tf_op jit(solution)/shard_map/ppermute | solution.py:323
  95.5 27.1 %copy-start = (bf16[1024,512]{1,0:T(8,128)(2,1)S(1)}, bf16[1024,512]{1,0:T(8,128)(2,1)}, u32[]{:S(2)}) copy-start(bf16[1024,512]{1,0:T(8,128)(2,1)} %weight_ref.1) | copy-start | bytes 3145732

commit v3 on v2

--- a/solution.py
+++ b/solution.py
@@ -12,7 +12,6 @@
 HEADS = 16
 HEAD_DIM = 64
 REACH = 3
-PIECES = 2
 BF = jnp.bfloat16
 F32 = jnp.float32
 VMEM = pl.BlockSpec(memory_space=pltpu.VMEM)
@@ -29,72 +28,107 @@
     return lax.broadcasted_iota(jnp.int32, shape, len(shape) - 1)
 
 
+def shift_rows(wide, out, rows, ref, edge_rows, lat, last):
+    n, span = out.shape[1], out.shape[2]
+    wide[:n, REACH : REACH + rows, :] = ref.astype(F32)
+    edge_rows = edge_rows.astype(F32)
+    nothing = jnp.zeros_like(edge_rows)
+    tail = 2 * REACH + rows
+    wide[:n, 0:REACH, :] = jnp.where(lat == 0, nothing, edge_rows)
+    wide[:n, REACH + rows : tail, :] = jnp.where(lat == last, nothing, edge_rows)
+    wide[:n, tail:, :] = jnp.zeros((n, wide.shape[1] - tail, wide.shape[2]), F32)
+    for a in range(3):
+        out[a] = wide[:n, a : a + span, :].astype(BF)
+
+
+def first_level(column, weight, span):
+    parts = [
+        jnp.concatenate([column(a, b), column(a, b + 1)], axis=0)
+        for a in range(3)
+        for b in range(3)
+    ]
+    first = silu(jnp.dot(jnp.concatenate(parts, axis=1), weight, preferred_element_type=F32))
+    return first[:span] + first[span:]
+
+
+def store_pair(pool, c, pair, rows, lat, last):
+    slabs = CB // 128
+    for s in range(slabs):
+        pool[c * slabs + s] = pair[:, 128 * s : 128 * (s + 1)]
+
+    @pl.when(lat == 0)
+    def _():
+        pool[c * slabs : (c + 1) * slabs, 0:2, :] = jnp.zeros((slabs, 2, 128), F32)
+
+    @pl.when(lat == last)
+    def _():
+        pool[c * slabs : (c + 1) * slabs, rows + 2 : rows + 4, :] = jnp.zeros((slabs, 2, 128), F32)
+
+
+def middle_kernel(
+    lat_ref, mid_ref, edge_ref, conv_a_hbm, shifted, pool, conv_a_ref, wide, sem
+):
+    copy = pltpu.make_async_copy(conv_a_hbm, conv_a_ref, sem)
+    copy.start()
+    lat = lat_ref[0]
+    last = lat_ref[1] - 1
+    cols, rows, _ = mid_ref.shape
+    shift_rows(wide, shifted, rows, mid_ref[...], edge_ref[...], lat, last)
+    copy.wait()
+    for c in range(cols // 2 - 2):
+        pair = first_level(
+            lambda a, b, c=c: shifted[a, 2 * c + 1 + b], conv_a_ref[...], shifted.shape[2]
+        )
+        store_pair(pool, c, pair, rows, lat, last)
+
+
 def conv_kernel(
-    lat_ref, mid_ref, low_ref, high_ref, edge_ref, gain_ref,
-    conv_a_hbm, conv_b_hbm, qkv_hbm,
+    lat_ref, shifted, pool_mid, conv_a_ref, low_ref, high_ref, gain_hbm, conv_b_hbm, qkv_hbm,
     tok_ref, out_ref,
-    conv_a_ref, conv_b_ref, qkv_ref, wide, shifted, pool_a, ready, pool_b, sems,
+    gain_ref, conv_b_ref, qkv_ref, wide, low, high, pool_side, ready, pool_b, sems,
 ):
     copies = [
-        pltpu.make_async_copy(conv_a_hbm, conv_a_ref, sems.at[0]),
-        pltpu.make_async_copy(conv_b_hbm, conv_b_ref, sems.at[1]),
+        pltpu.make_async_copy(conv_b_hbm, conv_b_ref, sems.at[0]),
+        pltpu.make_async_copy(gain_hbm, gain_ref, sems.at[1]),
         pltpu.make_async_copy(qkv_hbm, qkv_ref, sems.at[2]),
     ]
     for copy in copies:
         copy.start()
     lat = lat_ref[0]
     last = lat_ref[1] - 1
-    cols, rows, chans = mid_ref.shape
-    span = shifted.shape[2]
-    for ref, edge_rows, at in (
-        (low_ref, low_ref[:, rows:], 0),
-        (mid_ref, edge_ref[...], REACH),
-        (high_ref, high_ref[:, rows:], REACH + cols),
-    ):
-        n = ref.shape[0]
-        wide[at : at + n, REACH : REACH + rows, :] = ref[:, :rows].astype(F32)
-        rows_edge = edge_rows.astype(F32)
-        nothing = jnp.zeros_like(rows_edge)
-        wide[at : at + n, 0:REACH, :] = jnp.where(lat == 0, nothing, rows_edge)
-        wide[at : at + n, REACH + rows : 2 * REACH + rows, :] = jnp.where(
-            lat == last, nothing, rows_edge
-        )
-    tail = 2 * REACH + rows
-    wide[:, tail:, :] = jnp.zeros((wide.shape[0], wide.shape[1] - tail, chans), F32)
-    for a in range(3):
-        shifted[a] = wide[:, a : a + span, :].astype(BF)
-    copies[0].wait()
+    cols, span = shifted.shape[1], shifted.shape[2]
+    rows = low_ref.shape[1] - REACH
     slabs = CB // 128
     pooled_cols = cols // 2 + 2
+    pooled_rows = rows // 2
+    for ref, out in ((low_ref, low), (high_ref, high)):
+        shift_rows(wide, out, rows, ref[:, :rows], ref[:, rows:], lat, last)
+
+    def column(a, w):
+        if w < REACH:
+            return low[a, w]
+        if w < REACH + cols:
+            return shifted[a, w - REACH]
+        return high[a, w - REACH - cols]
+
+    def pooled(c):
+        if 2 <= c < pooled_cols - 2:
+            return pool_mid, c - 2
+        return pool_side, c if c < 2 else c - (pooled_cols - 4)
+
     for c in range(pooled_cols):
-        parts = [
-            shifted[a, 2 * c + b : 2 * c + b + 2].reshape(2 * span, chans)
-            for a in range(3)
-            for b in range(3)
-        ]
-        first = silu(
-            jnp.dot(jnp.concatenate(parts, axis=1), conv_a_ref[...], preferred_element_type=F32)
-        )
-        pair = first[:span] + first[span:]
-        for s in range(slabs):
-            pool_a[c * slabs + s] = pair[:, 128 * s : 128 * (s + 1)]
-    pooled_rows = rows // 2
-
-    @pl.when(lat == 0)
-    def _():
-        pool_a[:, 0:2, :] = jnp.zeros((pool_a.shape[0], 2, 128), F32)
-
-    @pl.when(lat == last)
-    def _():
-        pool_a[:, rows + 2 : rows + 4, :] = jnp.zeros((pool_a.shape[0], 2, 128), F32)
-
-    for c in range(pooled_cols):
+        pool, at = pooled(c)
+        if pool is pool_side:
+            pair = first_level(
+                lambda a, b, c=c: column(a, 2 * c + b), conv_a_ref[...], span
+            )
+            store_pair(pool, at, pair, rows, lat, last)
         for s in range(slabs):
             for a in range(3):
-                even = pool_a[c * slabs + s, pl.ds(2 * a, pooled_rows, stride=2), :]
-                odd = pool_a[c * slabs + s, pl.ds(2 * a + 1, pooled_rows, stride=2), :]
+                even = pool[at * slabs + s, pl.ds(2 * a, pooled_rows, stride=2), :]
+                odd = pool[at * slabs + s, pl.ds(2 * a + 1, pooled_rows, stride=2), :]
                 ready[a, c, :, 128 * s : 128 * (s + 1)] = ((even + odd) * 0.25).astype(BF)
-    copies[1].wait()
+    copies[0].wait()
     cols_b = cols // 2
     parts = [
         ready[a, b : b + cols_b].reshape(cols_b * pooled_rows, CB)
@@ -119,6 +153,7 @@
     tok_ref[...] = tokens
     centred = tokens - jnp.mean(tokens, axis=-1, keepdims=True)
     spread = jnp.mean(centred * centred, axis=-1, keepdims=True)
+    copies[1].wait()
     normed = (centred * lax.rsqrt(spread + 0.01) * gain_ref[...]).astype(BF)
     copies[2].wait()
     width = HEADS * HEAD_DIM
@@ -139,10 +174,10 @@
         out_ref[h + 1, count:] = jnp.where(below_half, turned[0][:half], q[half:]).astype(BF)
 
 
-def attention_kernel(first, final, *refs):
+def attention_kernel(first, final, pieces, *refs):
     refs = list(refs)
     q_ref = refs.pop(0)
-    kv_refs = [refs.pop(0) for _ in range(PIECES)]
+    kv_refs = [refs.pop(0) for _ in range(pieces)]
     held = None if first else (refs.pop(0), refs.pop(0))
     ones_vals = refs.pop()
     queries, acc_ref, top_ref = (None, None, None) if final else refs if first else (None, *refs)
@@ -163,7 +198,7 @@
         ones_vals[i] = jnp.where(mask_keys, one, kv[...])
     factor = HEAD_DIM ** (-0.5) * math.log2(math.e)
     block = rows // 2
-    units = [(at, i) for at in range(0, rows, block) for i in range(PIECES)]
+    units = [(at, i) for at in range(0, rows, block) for i in range(pieces)]
 
     def score(unit):
         at, i = unit
@@ -191,7 +226,7 @@
         part = jnp.dot(raised, ones_vals[i], preferred_element_type=F32)
         acc = part if acc is None else acc * jnp.exp2((top - new_top) * factor) + part
         top = new_top
-        if i < PIECES - 1:
+        if i < pieces - 1:
             continue
         if not final:
             acc_ref[:, at : at + block, :] = acc.reshape(2, block, 128)
@@ -215,15 +250,15 @@
     else:
         outs = tuple(([jax.ShapeDtypeStruct((2, rows, 128), BF)] if first else []) + state)
     return pl.pallas_call(
-        functools.partial(attention_kernel, first, final),
+        functools.partial(attention_kernel, first, final, len(pieces)),
         out_shape=outs,
-        in_specs=[VMEM] * (1 + PIECES + (0 if first else 2)),
+        in_specs=[VMEM] * (1 + len(pieces) + (0 if first else 2)),
         out_specs=VMEM if final else (VMEM,) * len(outs),
-        scratch_shapes=[pltpu.VMEM((PIECES, keys, 128), BF)],
+        scratch_shapes=[pltpu.VMEM((len(pieces), keys, 128), BF)],
         compiler_params=pltpu.CompilerParams(vmem_limit_bytes=24 * 2**20),
         cost_estimate=pl.CostEstimate(
-            flops=4 * 2 * rows * PIECES * keys * 256,
-            transcendentals=2 * rows * PIECES * keys,
+            flops=4 * 2 * rows * len(pieces) * keys * 256,
+            transcendentals=2 * rows * len(pieces) * keys,
             bytes_accessed=2**22,
         ),
         name="attention",
@@ -271,7 +306,6 @@
     field = surface_field.transpose(1, 0, 2)
     edge = edge.transpose(1, 0, 2)
 
-    wide_cols = cols + 2 * REACH
     span = -(-(rows + 4) // 16) * 16
     pooled_cols = cols // 2 + 2
     pooled_rows = rows // 2
@@ -279,6 +313,26 @@
     half = count // 2
     slabs = CB // 128
     where = jnp.stack([lat, jnp.int32(lat_count)]).astype(jnp.int32)
+
+    def in_hbm(value):
+        return pltpu.with_memory_space_constraint(value, pltpu.HBM)
+
+    shifted, pool_mid, conv_a_here = pl.pallas_call(
+        middle_kernel,
+        out_shape=(
+            jax.ShapeDtypeStruct((3, cols, span, chans), BF),
+            jax.ShapeDtypeStruct(((pooled_cols - 4) * slabs, span, 128), F32),
+            jax.ShapeDtypeStruct((9 * chans, CB), BF),
+        ),
+        in_specs=[SMEM, VMEM, VMEM, HBM],
+        out_specs=(VMEM,) * 3,
+        scratch_shapes=[
+            pltpu.VMEM((cols, span + 8, chans), F32),
+            pltpu.SemaphoreType.DMA,
+        ],
+        compiler_params=pltpu.CompilerParams(vmem_limit_bytes=16 * 2**20),
+        name="middle",
+    )(where, field, edge, in_hbm(conv_a.reshape(9 * chans, CB)))
     tokens, outgoing = pl.pallas_call(
         conv_kernel,
         out_shape=(
@@ -288,21 +342,22 @@
         in_specs=[SMEM] + [VMEM] * 5 + [HBM] * 3,
         out_specs=(VMEM, VMEM),
         scratch_shapes=[
-            pltpu.VMEM((9 * chans, CB), BF),
+            pltpu.VMEM((1, CB), F32),
             pltpu.VMEM((9 * CB, CB), BF),
             pltpu.VMEM(qkv_weight.shape, BF),
-            pltpu.VMEM((wide_cols, span + 8, chans), F32),
-            pltpu.VMEM((3, wide_cols, span, chans), BF),
-            pltpu.VMEM((pooled_cols * slabs, span, 128), F32),
+            pltpu.VMEM((REACH, span + 8, chans), F32),
+            pltpu.VMEM((3, REACH, span, chans), BF),
+            pltpu.VMEM((3, REACH, span, chans), BF),
+            pltpu.VMEM((4 * slabs, span, 128), F32),
             pltpu.VMEM((3, pooled_cols, pooled_rows, CB), BF),
             pltpu.VMEM((cols // 4 * slabs, pooled_rows, 128), F32),
             pltpu.SemaphoreType.DMA((3,)),
         ],
-        compiler_params=pltpu.CompilerParams(vmem_limit_bytes=40 * 2**20),
+        compiler_params=pltpu.CompilerParams(vmem_limit_bytes=32 * 2**20),
         name="convs",
     )(
-        where, field, low, high, edge, norm_gain.reshape(1, CB),
-        *[pltpu.with_memory_space_constraint(w, pltpu.HBM) for w in (conv_a.reshape(9 * chans, CB), conv_b.reshape(9 * CB, CB), qkv_weight)],
+        where, shifted, pool_mid, conv_a_here, low, high,
+        in_hbm(norm_gain.reshape(1, CB)), in_hbm(conv_b.reshape(9 * CB, CB)), in_hbm(qkv_weight),
     )
 
     residues = lon_count // HEADS
@@ -324,9 +379,10 @@
 
     near = beside(own, 1)
     near_back = beside(own, residues - 1)
+    queries, *held = attend(queries, [own], None, False)
+    own_other = other(own)
     far = beside(own, 2)
-    own_other = other(own)
-    queries, *held = attend(queries, [own, own_other], None, False)
+    held = attend(queries, [own_other], held, False)
     near_other = other(near)
     near_back_other = other(near_back)
     held = attend(queries, [near, near_back], held, False)

time: 124 us -> 116 us (0.935)
  waiting for transfers between devices: 19.9 us -> 7.93 us
  blocking collectives: 49.2 us -> 51.6 us
  Pallas kernels: 22.8 us -> 24.8 us
    pallas_call x4 -> x6, Pallas kernels: 12.2 us -> 16.8 us  [the longest x5 12.8 us: attend(): pl.pallas_call(functools.partial(attention_kernel, first, final, len(piec...]
    ppermute x1, waiting for transfers between devices: 4.51 us -> 0.01 us  [body(): high = lax.ppermute(columns(0), 'lon', backward)]
    ppermute x1, waiting for transfers between devices: 5.65 us -> 1.27 us  [body(): low = lax.ppermute(columns(cols - REACH), 'lon', forward)]
    ppermute x3, waiting for transfers between devices: 8.63 us -> 5.53 us  [beside(): return lax.ppermute(value, 'lon', pairs)]
    ppermute x1, starting transfers between devices: 0.13 us -> 2.89 us  [body(): low = lax.ppermute(columns(cols - REACH), 'lon', forward)]
    ppermute x1, starting transfers between devices: 25.1 us -> 22.3 us  [body(): high = lax.ppermute(columns(0), 'lon', backward)]
    pallas_call x1, Pallas kernels: 9.55 us -> 6.93 us  [body(): pl.pallas_call(conv_kernel, out_shape=(jax.ShapeDtypeStruct((count, CB),...]
    all_to_all x1, blocking collectives: 25.4 us -> 26.8 us  [body(): lax.all_to_all(outgoing, 'lon', 0, 0, axis_index_groups=groups, tiled=True)]
  transfers between devices with their start and end apart: 10 -> 10, of which waited for: 4 -> 5; matrix products, arithmetic and copies ran while one was open for 0% -> 0% of each run, Pallas kernels for 7% -> 12%
where the time goes in v3:
time: 116 us
  blocking collectives  51.6 us (44%)
  starting transfers between devices  29.8 us (26%)
  Pallas kernels  24.8 us (21%)
  waiting for transfers between devices  7.93 us (7%)
  local copies, waits for them, and re-layouts  1.23 us (1%)
    all_to_all x1, blocking collectives, body(): lax.all_to_all(outgoing, 'lon', 0, 0, axis_index_groups=groups, tiled=True)  26.8 us
    all_to_all x1, blocking collectives, body(): lax.all_to_all(attended.reshape(HEADS, half, 128), 'lon', 0, 0, axis_inde...  24.8 us
    ppermute x1, starting transfers between devices, body(): high = lax.ppermute(columns(0), 'lon', backward)  22.3 us
    pallas_call x5, Pallas kernels, attend(): pl.pallas_call(functools.partial(attention_kernel, first, final, len(piec...  12.8 us
    pallas_call x1, Pallas kernels, body(): pl.pallas_call(conv_kernel, out_shape=(jax.ShapeDtypeStruct((count, CB),...  6.93 us
    ppermute x3, waiting for transfers between devices, beside(): return lax.ppermute(value, 'lon', pairs)  5.53 us
    ppermute x3, starting transfers between devices, beside(): return lax.ppermute(value, 'lon', pairs)  4.36 us
    pallas_call x1, Pallas kernels, body(): pl.pallas_call(middle_kernel, out_shape=(jax.ShapeDtypeStruct((3, cols, s...  3.99 us
  transfers between devices with their start and end apart: 10, of which 5 were waited for; matrix products, arithmetic and copies ran while one was open for 0% of the time, Pallas kernels for 12%

profile of v3, /device:TPU:40, one launch (start us, length us, event | category | flops | bytes accessed | tf_op | source)
XLA Modules:
  0.0 115.5 jit_solution(17519893378148220672)
XLA Ops:
  0.0 1.1 copy.13
  1.2 0.1 collective-permute-start
  1.4 1.1 collective-permute-done
  2.5 2.9 %collective-permute-start.1 = (bf16[3,131,256]{2,1,0:T(8,128)(2,1)S(1)}, bf16[3,131,256]{2,1,0:T(8,128)(2,1)S(1)}, u32[]{:S(2)}, u32[]{:S(2)}) collective-permute-start(bf16[3,131,256]{2,1,0:T(8,128)(2,1)S(1)} %maximum_bitcast_fusion), channel_id=1, source_target_pairs={{0,2},{2,4},{4,6},{6,8},{8,10},{10,12},{12,14},{14,16},{16,18},{18... | collective-permute-start | bytes 603656 | tf_op jit(solution)/shard_map/ppermute | solution.py:304
  5.4 22.3 %collective-permute-start.2 = (bf16[3,131,256]{2,1,0:T(8,128)(2,1)S(1)}, bf16[3,131,256]{2,1,0:T(8,128)(2,1)S(1)}, u32[]{:S(2)}, u32[]{:S(2)}) collective-permute-start(bf16[3,131,256]{2,1,0:T(8,128)(2,1)S(1)} %maximum_bitcast_fusion.1), channel_id=1, source_target_pairs={{2,0},{4,2},{6,4},{8,6},{10,8},{12,10},{14,12},{16,14},{18,16},{20... | collective-permute-start | bytes 603656 | tf_op jit(solution)/shard_map/ppermute | solution.py:305
  27.8 0.1 pad_add_fusion.lat_ref
  27.9 4.0 %middle.1 = (bf16[3,8,144,256]{3,2,1,0:T(8,128)(2,1)S(1)}, f32[8,144,128]{2,1,0:T(8,128)S(1)}, bf16[2304,512]{1,0:T(8,128)(2,1)S(1)}) custom-call(s32[2]{0:T(128)S(1)} %pad_add_fusion.lat_ref, bf16[8,128,256]{2,1,0:T(8,128)(2,1)S(1)} %bitcast.14, bf16[8,3,256]{2,1,0:T(4,128)(2,1)S(1)} %bitcast.22, bf16[2304,512]{1,0:T(8,128)(2,1)} %bitcast.24), custom_call_target="tpu_custom_call" | custom-call | tf_op jit(solution)/shard_map/middle/pallas_call | solution.py:320
  31.9 1.3 %collective-permute-done.1.low_ref = bf16[3,131,256]{2,1,0:T(8,128)(2,1)S(1)} collective-permute-done((bf16[3,131,256]{2,1,0:T(8,128)(2,1)S(1)}, bf16[3,131,256]{2,1,0:T(8,128)(2,1)S(1)}, u32[]{:S(2)}, u32[]{:S(2)}) %collective-permute-start.1) | collective-permute-done | bytes 201248 | tf_op jit(solution)/shard_map/ppermute | solution.py:304
  33.1 0.0 collective-permute-done.2.high_ref
  33.1 6.9 %convs.1 = (f32[64,512]{1,0:T(8,128)S(1)}, bf16[16,96,128]{2,1,0:T(8,128)(2,1)S(1)}) custom-call(s32[2]{0:T(128)S(1)} %pad_add_fusion.lat_ref, bf16[3,8,144,256]{3,2,1,0:T(8,128)(2,1)S(1)} %get-tuple-element.19.shifted, f32[8,144,128]{2,1,0:T(8,128)S(1)} %get-tuple-element.20.pool_mid, bf16[2304,512]{1,0:T(8,128)(2,1)S(1)} %get-tuple-element.21.conv_a_ref, ...), custom_call_target="tpu_custom_call" | custom-call | tf_op jit(solution)/shard_map/convs/pallas_call | solution.py:336
  40.1 26.8 %all_to_all.10 = bf16[16,96,128]{2,1,0:T(8,128)(2,1)S(1)} all-to-all(bf16[16,96,128]{2,1,0:T(8,128)(2,1)S(1)} %get-tuple-element.22), channel_id=1, replica_groups={{0,2,4,6,8,10,12,14,16,18,20,22,24,26,28,30},{32,34,36,38,40,42,44,46,4..., dimensions={0} | all-to-all | bytes 786432 | tf_op jit(solution)/shard_map/all_to_all | solution.py:365
  66.9 0.3 collective-permute-start.5
  67.2 3.1 %collective-permute-start.7 = (bf16[1024,128]{1,0:T(8,128)(2,1)S(1)}, bf16[1024,128]{1,0:T(8,128)(2,1)S(1)}, u32[]{:S(2)}, u32[]{:S(2)}) collective-permute-start(bf16[1024,128]{1,0:T(8,128)(2,1)S(1)} %bitcast.16), channel_id=1, source_target_pairs={{0,96},{2,98},{4,100},{6,102},{8,104},{10,106},{12,108},{14,110},{... | collective-permute-start | bytes 786440 | tf_op jit(solution)/shard_map/ppermute | solution.py:375
  70.3 1.0 collective-permute-start.3
  71.3 0.0 collective-permute-start.9
  71.3 1.6 %attention.5 = (bf16[2,512,128]{2,1,0:T(8,128)(2,1)S(1)}, f32[2,512,128]{2,1,0:T(8,128)S(1)}, f32[2,512,128]{2,1,0:T(8,128)S(1)}) custom-call(bf16[512,128]{1,0:T(8,128)(2,1)S(1)} %bitcast.21, bf16[1024,128]{1,0:T(8,128)(2,1)S(1)} %bitcast.19), custom_call_target="tpu_custom_call" | custom-call | flops 1073741824 | bytes 4194304 | tf_op jit(solution)/shard_map/attention/pallas_call | solution.py:252
  72.9 1.7 %collective-permute-done.5.refs_1_ = bf16[1024,128]{1,0:T(8,128)(2,1)S(1)} collective-permute-done((bf16[1024,128]{1,0:T(8,128)(2,1)S(1)}, bf16[1024,128]{1,0:T(8,128)(2,1)S(1)}, u32[]{:S(2)}, u32[]{:S(2)}) %collective-permute-start.5) | collective-permute-done | bytes 262176 | tf_op jit(solution)/shard_map/ppermute | solution.py:375
  74.6 0.0 collective-permute-start.6
  74.6 2.4 %collective-permute-done.7.refs_2_ = bf16[1024,128]{1,0:T(8,128)(2,1)S(1)} collective-permute-done((bf16[1024,128]{1,0:T(8,128)(2,1)S(1)}, bf16[1024,128]{1,0:T(8,128)(2,1)S(1)}, u32[]{:S(2)}, u32[]{:S(2)}) %collective-permute-start.7) | collective-permute-done | bytes 262176 | tf_op jit(solution)/shard_map/ppermute | solution.py:375
  77.0 0.0 collective-permute-start.8
  77.0 1.4 %collective-permute-done.3.refs_1_ = bf16[1024,128]{1,0:T(8,128)(2,1)S(1)} collective-permute-done((bf16[1024,128]{1,0:T(8,128)(2,1)S(1)}, bf16[1024,128]{1,0:T(8,128)(2,1)S(1)}, u32[]{:S(2)}, u32[]{:S(2)}) %collective-permute-start.3) | collective-permute-done | bytes 262176 | tf_op jit(solution)/shard_map/ppermute | solution.py:375
  78.4 0.0 collective-permute-start.4
  78.4 0.0 collective-permute-done.9.refs_1_
  78.4 1.8 %attention.6 = (f32[2,512,128]{2,1,0:T(8,128)S(1)}, f32[2,512,128]{2,1,0:T(8,128)S(1)}) custom-call(bf16[2,512,128]{2,1,0:T(8,128)(2,1)S(1)} %get-tuple-element.23.refs_0_, bf16[1024,128]{1,0:T(8,128)(2,1)S(1)} %collective-permute-done.9.refs_1_, f32[2,512,128]{2,1,0:T(8,128)S(1)} %get-tuple-element.24.refs_2_, f32[2,512,128]{2,1,0:T(8,128)S(1)} %get-tuple-element.25.refs_3_), custom_call_target="tpu_custom_call" | custom-call | flops 1073741824 | bytes 4194304 | tf_op jit(solution)/shard_map/attention/pallas_call | solution.py:252
  80.2 3.1 %attention.7 = (f32[2,512,128]{2,1,0:T(8,128)S(1)}, f32[2,512,128]{2,1,0:T(8,128)S(1)}) custom-call(bf16[2,512,128]{2,1,0:T(8,128)(2,1)S(1)} %get-tuple-element.23.refs_0_, bf16[1024,128]{1,0:T(8,128)(2,1)S(1)} %collective-permute-done.5.refs_1_, bf16[1024,128]{1,0:T(8,128)(2,1)S(1)} %collective-permute-done.7.refs_2_, ...), custom_call_target="tpu_custom_call" | custom-call | flops 2147483648 | bytes 4194304 | tf_op jit(solution)/shard_map/attention/pallas_call | solution.py:252
  83.3 0.0 collective-permute-done.6.refs_1_
  83.3 0.0 collective-permute-done.8.refs_2_
  83.3 3.1 %attention.8 = (f32[2,512,128]{2,1,0:T(8,128)S(1)}, f32[2,512,128]{2,1,0:T(8,128)S(1)}) custom-call(bf16[2,512,128]{2,1,0:T(8,128)(2,1)S(1)} %get-tuple-element.23.refs_0_, bf16[1024,128]{1,0:T(8,128)(2,1)S(1)} %collective-permute-done.6.refs_1_, bf16[1024,128]{1,0:T(8,128)(2,1)S(1)} %collective-permute-done.8.refs_2_, ...), custom_call_target="tpu_custom_call" | custom-call | flops 2147483648 | bytes 4194304 | tf_op jit(solution)/shard_map/attention/pallas_call | solution.py:252
  86.4 0.0 collective-permute-done.4.refs_2_
  86.4 0.0 copy-start
  86.4 3.3 %attention.9 = bf16[512,128]{1,0:T(8,128)(2,1)S(1)} custom-call(bf16[2,512,128]{2,1,0:T(8,128)(2,1)S(1)} %get-tuple-element.23.refs_0_, bf16[1024,128]{1,0:T(8,128)(2,1)S(1)} %collective-permute-done.3.refs_1_, bf16[1024,128]{1,0:T(8,128)(2,1)S(1)} %collective-permute-done.4.refs_2_, f32[2,512,128]{2,1,0:T(8,128)S(1)} %get-tuple-element.30.refs_3_, ...), custom_call_target="tpu_custom_call" | custom-call | flops 2147483648 | bytes 4194304 | tf_op jit(solution)/shard_map/attention/pallas_call | solution.py:252
  89.7 24.8 %all_to_all.11.back_ref = bf16[16,32,128]{2,1,0:T(8,128)(2,1)S(1)} all-to-all(bf16[16,32,128]{2,1,0:T(8,128)(2,1)S(1)} %bitcast.20), channel_id=1, replica_groups={{0,2,4,6,8,10,12,14,16,18,20,22,24,26,28,30},{32,34,36,38,40,42,44,46,4..., dimensions={0} | all-to-all | bytes 262144 | tf_op jit(solution)/shard_map/all_to_all | solution.py:392
  114.5 0.0 copy-done
  114.5 1.1 mix.1
  (7 shorter events, 0.1 us)
Async XLA Ops:
  1.2 1.3 %collective-permute-start = (bf16[3,8,256]{2,0,1:T(4,128)(2,1)S(1)}, bf16[3,8,256]{2,0,1:T(4,128)(2,1)S(1)}, u32[]{:S(2)}, u32[]{:S(2)}) collective-permute-start(bf16[3,8,256]{2,0,1:T(4,128)(2,1)S(1)} %constant_dynamic-slice_fusion), channel_id=1, source_target_pairs={{0,1},{1,0},{2,3},{3,2},{4,5},{5,4},{6,7},{7,6},{8,9},{9,8},{10,11... | collective-permute-start | bytes 36872 | tf_op jit(solution)/shard_map/ppermute | solution.py:296
  2.5 30.6 %collective-permute-start.1 = (bf16[3,131,256]{2,1,0:T(8,128)(2,1)S(1)}, bf16[3,131,256]{2,1,0:T(8,128)(2,1)S(1)}, u32[]{:S(2)}, u32[]{:S(2)}) collective-permute-start(bf16[3,131,256]{2,1,0:T(8,128)(2,1)S(1)} %maximum_bitcast_fusion), channel_id=1, source_target_pairs={{0,2},{2,4},{4,6},{6,8},{8,10},{10,12},{12,14},{14,16},{16,18},{18... | collective-permute-start | bytes 603656 | tf_op jit(solution)/shard_map/ppermute | solution.py:304
  5.4 27.7 %collective-permute-start.2 = (bf16[3,131,256]{2,1,0:T(8,128)(2,1)S(1)}, bf16[3,131,256]{2,1,0:T(8,128)(2,1)S(1)}, u32[]{:S(2)}, u32[]{:S(2)}) collective-permute-start(bf16[3,131,256]{2,1,0:T(8,128)(2,1)S(1)} %maximum_bitcast_fusion.1), channel_id=1, source_target_pairs={{2,0},{4,2},{6,4},{8,6},{10,8},{12,10},{14,12},{16,14},{18,16},{20... | collective-permute-start | bytes 603656 | tf_op jit(solution)/shard_map/ppermute | solution.py:305
  66.9 7.7 %collective-permute-start.5 = (bf16[1024,128]{1,0:T(8,128)(2,1)S(1)}, bf16[1024,128]{1,0:T(8,128)(2,1)S(1)}, u32[]{:S(2)}, u32[]{:S(2)}) collective-permute-start(bf16[1024,128]{1,0:T(8,128)(2,1)S(1)} %bitcast.15), channel_id=1, source_target_pairs={{0,32},{2,34},{4,36},{6,38},{8,40},{10,42},{12,44},{14,46},{16,48}... | collective-permute-start | bytes 786440 | tf_op jit(solution)/shard_map/ppermute | solution.py:375
  67.2 9.8 %collective-permute-start.7 = (bf16[1024,128]{1,0:T(8,128)(2,1)S(1)}, bf16[1024,128]{1,0:T(8,128)(2,1)S(1)}, u32[]{:S(2)}, u32[]{:S(2)}) collective-permute-start(bf16[1024,128]{1,0:T(8,128)(2,1)S(1)} %bitcast.16), channel_id=1, source_target_pairs={{0,96},{2,98},{4,100},{6,102},{8,104},{10,106},{12,108},{14,110},{... | collective-permute-start | bytes 786440 | tf_op jit(solution)/shard_map/ppermute | solution.py:375
  70.3 8.2 %collective-permute-start.3 = (bf16[1024,128]{1,0:T(8,128)(2,1)S(1)}, bf16[1024,128]{1,0:T(8,128)(2,1)S(1)}, u32[]{:S(2)}, u32[]{:S(2)}) collective-permute-start(bf16[1024,128]{1,0:T(8,128)(2,1)S(1)} %bitcast.17), channel_id=1, source_target_pairs={{0,64},{2,66},{4,68},{6,70},{8,72},{10,74},{12,76},{14,78},{16,80}... | collective-permute-start | bytes 786440 | tf_op jit(solution)/shard_map/ppermute | solution.py:375
  71.3 7.2 %collective-permute-start.9 = (bf16[1024,128]{1,0:T(8,128)(2,1)S(1)}, bf16[1024,128]{1,0:T(8,128)(2,1)S(1)}, u32[]{:S(2)}, u32[]{:S(2)}) collective-permute-start(bf16[1024,128]{1,0:T(8,128)(2,1)S(1)} %bitcast.18), channel_id=1, source_target_pairs={{0,1},{1,0},{2,3},{3,2},{4,5},{5,4},{6,7},{7,6},{8,9},{9,8},{10,11... | collective-permute-start | bytes 786440 | tf_op jit(solution)/shard_map/ppermute | solution.py:378
  74.6 8.7 %collective-permute-start.6 = (bf16[1024,128]{1,0:T(8,128)(2,1)S(1)}, bf16[1024,128]{1,0:T(8,128)(2,1)S(1)}, u32[]{:S(2)}, u32[]{:S(2)}) collective-permute-start(bf16[1024,128]{1,0:T(8,128)(2,1)S(1)} %collective-permute-done.5.refs_1_), channel_id=1, source_target_pairs={{0,1},{1,0},{2,3},{3,2},{4,5},{5,4},{6,7},{7,6},{8,9},{9,8},{10,11... | collective-permute-start | bytes 786440 | tf_op jit(solution)/shard_map/ppermute | solution.py:378
  77.0 6.3 %collective-permute-start.8 = (bf16[1024,128]{1,0:T(8,128)(2,1)S(1)}, bf16[1024,128]{1,0:T(8,128)(2,1)S(1)}, u32[]{:S(2)}, u32[]{:S(2)}) collective-permute-start(bf16[1024,128]{1,0:T(8,128)(2,1)S(1)} %collective-permute-done.7.refs_2_), channel_id=1, source_target_pairs={{0,1},{1,0},{2,3},{3,2},{4,5},{5,4},{6,7},{7,6},{8,9},{9,8},{10,11... | collective-permute-start | bytes 786440 | tf_op jit(solution)/shard_map/ppermute | solution.py:378
  78.4 8.0 %collective-permute-start.4 = (bf16[1024,128]{1,0:T(8,128)(2,1)S(1)}, bf16[1024,128]{1,0:T(8,128)(2,1)S(1)}, u32[]{:S(2)}, u32[]{:S(2)}) collective-permute-start(bf16[1024,128]{1,0:T(8,128)(2,1)S(1)} %collective-permute-done.3.refs_1_), channel_id=1, source_target_pairs={{0,1},{1,0},{2,3},{3,2},{4,5},{5,4},{6,7},{7,6},{8,9},{9,8},{10,11... | collective-permute-start | bytes 786440 | tf_op jit(solution)/shard_map/ppermute | solution.py:378
  86.4 28.1 %copy-start = (bf16[1024,512]{1,0:T(8,128)(2,1)S(1)}, bf16[1024,512]{1,0:T(8,128)(2,1)}, u32[]{:S(2)}) copy-start(bf16[1024,512]{1,0:T(8,128)(2,1)} %weight_ref.1) | copy-start | bytes 3145732

commit v4 on v3

--- a/solution.py
+++ b/solution.py
@@ -30,8 +30,7 @@
 
 def shift_rows(wide, out, rows, ref, edge_rows, lat, last):
     n, span = out.shape[1], out.shape[2]
-    wide[:n, REACH : REACH + rows, :] = ref.astype(F32)
-    edge_rows = edge_rows.astype(F32)
+    wide[:n, REACH : REACH + rows, :] = ref
     nothing = jnp.zeros_like(edge_rows)
     tail = 2 * REACH + rows
     wide[:n, 0:REACH, :] = jnp.where(lat == 0, nothing, edge_rows)
@@ -41,14 +40,17 @@
         out[a] = wide[:n, a : a + span, :].astype(BF)
 
 
-def first_level(column, weight, span):
+def first_level(column, firsts, weight, span):
     parts = [
-        jnp.concatenate([column(a, b), column(a, b + 1)], axis=0)
+        jnp.concatenate([column(a, w + b + n) for w in firsts for n in (0, 1)], axis=0)
         for a in range(3)
         for b in range(3)
     ]
     first = silu(jnp.dot(jnp.concatenate(parts, axis=1), weight, preferred_element_type=F32))
-    return first[:span] + first[span:]
+    return [
+        first[2 * n * span : (2 * n + 1) * span] + first[(2 * n + 1) * span : (2 * n + 2) * span]
+        for n in range(len(firsts))
+    ]
 
 
 def store_pair(pool, c, pair, rows, lat, last):
@@ -65,44 +67,64 @@
         pool[c * slabs : (c + 1) * slabs, rows + 2 : rows + 4, :] = jnp.zeros((slabs, 2, 128), F32)
 
 
+def pool_rows(pool, at, ready, c):
+    slabs = CB // 128
+    count = ready.shape[2]
+    for s in range(slabs):
+        for a in range(3):
+            even = pool[at * slabs + s, pl.ds(2 * a, count, stride=2), :]
+            odd = pool[at * slabs + s, pl.ds(2 * a + 1, count, stride=2), :]
+            ready[a, c, :, 128 * s : 128 * (s + 1)] = ((even + odd) * 0.25).astype(BF)
+
+
 def middle_kernel(
-    lat_ref, mid_ref, edge_ref, conv_a_hbm, shifted, pool, conv_a_ref, wide, sem
-):
-    copy = pltpu.make_async_copy(conv_a_hbm, conv_a_ref, sem)
-    copy.start()
-    lat = lat_ref[0]
-    last = lat_ref[1] - 1
-    cols, rows, _ = mid_ref.shape
-    shift_rows(wide, shifted, rows, mid_ref[...], edge_ref[...], lat, last)
-    copy.wait()
-    for c in range(cols // 2 - 2):
-        pair = first_level(
-            lambda a, b, c=c: shifted[a, 2 * c + 1 + b], conv_a_ref[...], shifted.shape[2]
-        )
-        store_pair(pool, c, pair, rows, lat, last)
-
-
-def conv_kernel(
-    lat_ref, shifted, pool_mid, conv_a_ref, low_ref, high_ref, gain_hbm, conv_b_hbm, qkv_hbm,
-    tok_ref, out_ref,
-    gain_ref, conv_b_ref, qkv_ref, wide, low, high, pool_side, ready, pool_b, sems,
+    lat_ref, mid_ref, edge_ref, conv_a_hbm, conv_b_hbm, qkv_hbm,
+    shifted, ready, conv_a_ref, conv_b_ref, qkv_ref,
+    wide, pool, sems,
 ):
     copies = [
-        pltpu.make_async_copy(conv_b_hbm, conv_b_ref, sems.at[0]),
-        pltpu.make_async_copy(gain_hbm, gain_ref, sems.at[1]),
+        pltpu.make_async_copy(conv_a_hbm, conv_a_ref, sems.at[0]),
+        pltpu.make_async_copy(conv_b_hbm, conv_b_ref, sems.at[1]),
         pltpu.make_async_copy(qkv_hbm, qkv_ref, sems.at[2]),
     ]
     for copy in copies:
         copy.start()
     lat = lat_ref[0]
     last = lat_ref[1] - 1
+    cols, rows, _ = mid_ref.shape
+    shift_rows(
+        wide, shifted, rows, mid_ref[...].astype(F32), edge_ref[...].astype(F32), lat, last
+    )
+    copies[0].wait()
+    firsts = [2 * c + 1 for c in range(cols // 2 - 2)]
+    pairs = first_level(lambda a, w: shifted[a, w], firsts, conv_a_ref[...], shifted.shape[2])
+    for c, pair in enumerate(pairs):
+        store_pair(pool, c, pair, rows, lat, last)
+        pool_rows(pool, c, ready, c)
+    copies[1].wait()
+    copies[2].wait()
+
+
+def conv_kernel(
+    lat_ref, shifted, ready_mid, conv_a_ref, conv_b_ref, qkv_ref, pair_ref, next_ref, gain_ref,
+    tok_ref, out_ref,
+    wide, low, high, pool_side, ready, pool_b,
+):
+    lat = lat_ref[0]
+    last = lat_ref[1] - 1
     cols, span = shifted.shape[1], shifted.shape[2]
-    rows = low_ref.shape[1] - REACH
+    rows = pair_ref.shape[1] - REACH
+    even = lat_ref[2] == 0
     slabs = CB // 128
     pooled_cols = cols // 2 + 2
     pooled_rows = rows // 2
-    for ref, out in ((low_ref, low), (high_ref, high)):
-        shift_rows(wide, out, rows, ref[:, :rows], ref[:, rows:], lat, last)
+    of_pair = pair_ref[...].astype(F32)
+    of_next = next_ref[...].astype(F32)
+    for out, value in (
+        (low, jnp.where(even, of_next, of_pair)),
+        (high, jnp.where(even, of_pair, of_next)),
+    ):
+        shift_rows(wide, out, rows, value[:, :rows], value[:, rows:], lat, last)
 
     def column(a, w):
         if w < REACH:
@@ -111,27 +133,20 @@
             return shifted[a, w - REACH]
         return high[a, w - REACH - cols]
 
-    def pooled(c):
+    for at, group in ((0, (0, 1)), (2, (pooled_cols - 2, pooled_cols - 1))):
+        pairs = first_level(column, [2 * c for c in group], conv_a_ref[...], span)
+        for n, pair in enumerate(pairs):
+            store_pair(pool_side, at + n, pair, rows, lat, last)
+            pool_rows(pool_side, at + n, ready, at + n)
+
+    def pooled(a, c):
         if 2 <= c < pooled_cols - 2:
-            return pool_mid, c - 2
-        return pool_side, c if c < 2 else c - (pooled_cols - 4)
-
-    for c in range(pooled_cols):
-        pool, at = pooled(c)
-        if pool is pool_side:
-            pair = first_level(
-                lambda a, b, c=c: column(a, 2 * c + b), conv_a_ref[...], span
-            )
-            store_pair(pool, at, pair, rows, lat, last)
-        for s in range(slabs):
-            for a in range(3):
-                even = pool[at * slabs + s, pl.ds(2 * a, pooled_rows, stride=2), :]
-                odd = pool[at * slabs + s, pl.ds(2 * a + 1, pooled_rows, stride=2), :]
-                ready[a, c, :, 128 * s : 128 * (s + 1)] = ((even + odd) * 0.25).astype(BF)
-    copies[0].wait()
+            return ready_mid[a, c - 2]
+        return ready[a, c if c < 2 else c - (pooled_cols - 4)]
+
     cols_b = cols // 2
     parts = [
-        ready[a, b : b + cols_b].reshape(cols_b * pooled_rows, CB)
+        jnp.concatenate([pooled(a, c + b) for c in range(cols_b)], axis=0)
         for a in range(3)
         for b in range(3)
     ]
@@ -153,9 +168,7 @@
     tok_ref[...] = tokens
     centred = tokens - jnp.mean(tokens, axis=-1, keepdims=True)
     spread = jnp.mean(centred * centred, axis=-1, keepdims=True)
-    copies[1].wait()
     normed = (centred * lax.rsqrt(spread + 0.01) * gain_ref[...]).astype(BF)
-    copies[2].wait()
     width = HEADS * HEAD_DIM
     count = tokens.shape[0]
     half = count // 2
@@ -177,11 +190,17 @@
 def attention_kernel(first, final, pieces, *refs):
     refs = list(refs)
     q_ref = refs.pop(0)
-    kv_refs = [refs.pop(0) for _ in range(pieces)]
+    kv_refs = [[refs.pop(0) for _ in range(n)] for n in pieces]
+    pieces = len(kv_refs)
     held = None if first else (refs.pop(0), refs.pop(0))
     ones_vals = refs.pop()
     queries, acc_ref, top_ref = (None, None, None) if final else refs if first else (None, *refs)
-    keys = kv_refs[0].shape[0]
+    keys = ones_vals.shape[1]
+
+    def piece(i):
+        parts = [ref[...] for ref in kv_refs[i]]
+        return parts[0] if len(parts) == 1 else jnp.concatenate(parts, axis=0)
+
     mask_keys = lanes_of((keys, 128)) < HEAD_DIM
     if first:
         rows = q_ref.shape[0]
@@ -194,8 +213,8 @@
         queries = q_ref
         rows = q_ref.shape[1]
     one = jnp.ones((keys, 128), BF)
-    for i, kv in enumerate(kv_refs):
-        ones_vals[i] = jnp.where(mask_keys, one, kv[...])
+    for i in range(pieces):
+        ones_vals[i] = jnp.where(mask_keys, one, piece(i))
     factor = HEAD_DIM ** (-0.5) * math.log2(math.e)
     block = rows // 2
     units = [(at, i) for at in range(0, rows, block) for i in range(pieces)]
@@ -204,7 +223,7 @@
         at, i = unit
         return lax.dot_general(
             queries[:, at : at + block, :].reshape(2 * block, 128),
-            kv_refs[i][...],
+            piece(i),
             (((1,), (1,)), ((), ())),
             preferred_element_type=F32,
         )
@@ -243,16 +262,17 @@
 def attend(queries, pieces, held, final):
     first = held is None
     rows = queries.shape[0] if first else queries.shape[1]
-    keys = pieces[0].shape[0]
+    keys = sum(part.shape[0] for part in pieces[0])
+    parts = [part for piece in pieces for part in piece]
     state = [jax.ShapeDtypeStruct((2, rows, 128), F32)] * 2
     if final:
         outs = jax.ShapeDtypeStruct((rows, 128), BF)
     else:
         outs = tuple(([jax.ShapeDtypeStruct((2, rows, 128), BF)] if first else []) + state)
     return pl.pallas_call(
-        functools.partial(attention_kernel, first, final, len(pieces)),
+        functools.partial(attention_kernel, first, final, [len(piece) for piece in pieces]),
         out_shape=outs,
-        in_specs=[VMEM] * (1 + len(pieces) + (0 if first else 2)),
+        in_specs=[VMEM] * (1 + len(parts) + (0 if first else 2)),
         out_specs=VMEM if final else (VMEM,) * len(outs),
         scratch_shapes=[pltpu.VMEM((len(pieces), keys, 128), BF)],
         compiler_params=pltpu.CompilerParams(vmem_limit_bytes=24 * 2**20),
@@ -262,7 +282,7 @@
             bytes_accessed=2**22,
         ),
         name="attention",
-    )(queries, *pieces, *(held or ()))
+    )(queries, *parts, *(held or ()))
 
 
 def out_kernel(back_ref, tok_ref, weight_ref, out_ref):
@@ -284,13 +304,22 @@
     out_ref[...] = jnp.stack(columns, axis=1).astype(BF)
 
 
+def swaps(offset, count, stride):
+    pairs = []
+    for i in range(0, count, 2):
+        one, two = offset(i) % count, (offset(i) + 1) % count
+        for s in range(stride):
+            pairs += [(one * stride + s, two * stride + s), (two * stride + s, one * stride + s)]
+    return pairs
+
+
 def body(surface_field, conv_a, conv_b, norm_gain, qkv_weight, out_weight):
     lon_count = lax.axis_size("lon")
     lat_count = lax.axis_size("lat")
     lat = lax.axis_index("lat")
     rows, cols, chans = surface_field.shape
-    forward = [(i, (i + 1) % lon_count) for i in range(lon_count)]
-    backward = [(target, source) for source, target in forward]
+    lon = lax.axis_index("lon")
+    even = lon % 2 == 0
     swap = [(c, (c + 1) % lat_count) for c in range(lat_count)]
     first_row = jnp.where(lat == 0, rows - REACH, 0)
     edge = lax.ppermute(
@@ -301,8 +330,11 @@
         beyond = jnp.concatenate([surface_field[:, at : at + REACH], edge[:, at : at + REACH]])
         return beyond.transpose(1, 0, 2)
 
-    low = lax.ppermute(columns(cols - REACH), "lon", forward)
-    high = lax.ppermute(columns(0), "lon", backward)
+    above, below = columns(cols - REACH), columns(0)
+    of_pair = lax.ppermute(jnp.where(even, above, below), "lon", swaps(lambda i: i, lon_count, 1))
+    of_next = lax.ppermute(
+        jnp.where(even, below, above), "lon", swaps(lambda i: i + 1, lon_count, 1)
+    )
     field = surface_field.transpose(1, 0, 2)
     edge = edge.transpose(1, 0, 2)
 
@@ -312,53 +344,48 @@
     count = (rows // 4) * (cols // 4)
     half = count // 2
     slabs = CB // 128
-    where = jnp.stack([lat, jnp.int32(lat_count)]).astype(jnp.int32)
+    where = jnp.stack([lat, jnp.int32(lat_count), lon % 2]).astype(jnp.int32)
 
     def in_hbm(value):
         return pltpu.with_memory_space_constraint(value, pltpu.HBM)
 
-    shifted, pool_mid, conv_a_here = pl.pallas_call(
+    weights = (conv_a.reshape(9 * chans, CB), conv_b.reshape(9 * CB, CB), qkv_weight)
+    shifted, ready_mid, *here = pl.pallas_call(
         middle_kernel,
         out_shape=(
             jax.ShapeDtypeStruct((3, cols, span, chans), BF),
-            jax.ShapeDtypeStruct(((pooled_cols - 4) * slabs, span, 128), F32),
-            jax.ShapeDtypeStruct((9 * chans, CB), BF),
-        ),
-        in_specs=[SMEM, VMEM, VMEM, HBM],
-        out_specs=(VMEM,) * 3,
+            jax.ShapeDtypeStruct((3, pooled_cols - 4, pooled_rows, CB), BF),
+        )
+        + tuple(jax.ShapeDtypeStruct(w.shape, BF) for w in weights),
+        in_specs=[SMEM, VMEM, VMEM] + [HBM] * 3,
+        out_specs=(VMEM,) * 5,
         scratch_shapes=[
             pltpu.VMEM((cols, span + 8, chans), F32),
-            pltpu.SemaphoreType.DMA,
+            pltpu.VMEM(((pooled_cols - 4) * slabs, span, 128), F32),
+            pltpu.SemaphoreType.DMA((3,)),
         ],
-        compiler_params=pltpu.CompilerParams(vmem_limit_bytes=16 * 2**20),
+        compiler_params=pltpu.CompilerParams(vmem_limit_bytes=24 * 2**20),
         name="middle",
-    )(where, field, edge, in_hbm(conv_a.reshape(9 * chans, CB)))
+    )(where, field, edge, *[in_hbm(w) for w in weights])
     tokens, outgoing = pl.pallas_call(
         conv_kernel,
         out_shape=(
             jax.ShapeDtypeStruct((count, CB), F32),
             jax.ShapeDtypeStruct((HEADS, count + half, 128), BF),
         ),
-        in_specs=[SMEM] + [VMEM] * 5 + [HBM] * 3,
+        in_specs=[SMEM] + [VMEM] * 8,
         out_specs=(VMEM, VMEM),
         scratch_shapes=[
-            pltpu.VMEM((1, CB), F32),
-            pltpu.VMEM((9 * CB, CB), BF),
-            pltpu.VMEM(qkv_weight.shape, BF),
             pltpu.VMEM((REACH, span + 8, chans), F32),
             pltpu.VMEM((3, REACH, span, chans), BF),
             pltpu.VMEM((3, REACH, span, chans), BF),
             pltpu.VMEM((4 * slabs, span, 128), F32),
-            pltpu.VMEM((3, pooled_cols, pooled_rows, CB), BF),
+            pltpu.VMEM((3, 4, pooled_rows, CB), BF),
             pltpu.VMEM((cols // 4 * slabs, pooled_rows, 128), F32),
-            pltpu.SemaphoreType.DMA((3,)),
         ],
-        compiler_params=pltpu.CompilerParams(vmem_limit_bytes=32 * 2**20),
+        compiler_params=pltpu.CompilerParams(vmem_limit_bytes=24 * 2**20),
         name="convs",
-    )(
-        where, shifted, pool_mid, conv_a_here, low, high,
-        in_hbm(norm_gain.reshape(1, CB)), in_hbm(conv_b.reshape(9 * CB, CB)), in_hbm(qkv_weight),
-    )
+    )(where, shifted, ready_mid, *here, of_pair, of_next, norm_gain.reshape(1, CB))
 
     residues = lon_count // HEADS
     groups = [[r * HEADS + h for h in range(HEADS)] for r in range(residues)]
@@ -366,29 +393,31 @@
     queries = arrived[:, count:].reshape(HEADS * half, 128)
     own = arrived[:, :count].reshape(HEADS * count, 128)
 
-    def beside(value, d):
-        pairs = [
-            (r * HEADS + h, (r + d) % residues * HEADS + h)
-            for r in range(residues)
-            for h in range(HEADS)
-        ]
-        return lax.ppermute(value, "lon", pairs)
-
     def other(value):
         return lax.ppermute(value, "lat", swap)
 
-    near = beside(own, 1)
-    near_back = beside(own, residues - 1)
-    queries, *held = attend(queries, [own], None, False)
+    def pair_swap(value):
+        return lax.ppermute(value, "lon", swaps(lambda i: i, residues, HEADS))
+
+    def next_swap(value):
+        return lax.ppermute(value, "lon", swaps(lambda i: i + 1, residues, HEADS))
+
+    near = pair_swap(own)
+    near_back = next_swap(own)
+    queries, *held = attend(queries, [(own,)], None, False)
     own_other = other(own)
-    far = beside(own, 2)
-    held = attend(queries, [own_other], held, False)
+    held = attend(queries, [(own_other,)], held, False)
+    middle = own.shape[0] // 2
+    far_a = pair_swap(near_back[:middle])
+    far_b = next_swap(near[middle:])
     near_other = other(near)
     near_back_other = other(near_back)
-    held = attend(queries, [near, near_back], held, False)
-    far_other = other(far)
-    held = attend(queries, [near_other, near_back_other], held, False)
-    attended = attend(queries, [far, far_other], held, True)
+    held = attend(queries, [(near,), (near_back,)], held, False)
+    held = attend(queries, [(near_other,), (near_back_other,)], held, False)
+    far_a_other = other(far_a)
+    far_b_other = other(far_b)
+    held = attend(queries, [(far_a, far_b)], held, False)
+    attended = attend(queries, [(far_a_other, far_b_other)], held, True)
     returned = lax.all_to_all(
         attended.reshape(HEADS, half, 128), "lon", 0, 0, axis_index_groups=groups, tiled=True
     )

time: 116 us -> 114 us (0.983)
  blocking collectives: 51.6 us -> 48.7 us
    all_to_all x1, blocking collectives: 24.8 us -> 21.9 us  [body(): lax.all_to_all(attended.reshape(HEADS, half, 128), 'lon', 0, 0, axis_inde...]
    pallas_call x5 -> x6, Pallas kernels: 12.8 us -> 13.4 us  [attend(): pl.pallas_call(functools.partial(attention_kernel, first, final, [len(pie...]
    ppermute x5 -> x6, starting transfers between devices: 29.6 us -> 29.1 us  [the longest x1 22.4 us: body(): lax.ppermute(jnp.where(even, below, above), 'lon', swaps(lambda i: i + 1,...]
    ppermute x5 -> x6, waiting for transfers between devices: 6.8 us -> 6.71 us  [the longest x2 3.35 us: next_swap(): return lax.ppermute(value, 'lon', swaps(lambda i: i + 1, residues, HEADS))]
  transfers between devices with their start and end apart: 10 -> 12, of which waited for: 5 -> 4; matrix products, arithmetic and copies ran while one was open for 0% -> 0% of each run, Pallas kernels for 12% -> 14%
where the time goes in v4:
time: 114 us
  blocking collectives  48.7 us (43%)
  starting transfers between devices  30.3 us (27%)
  Pallas kernels  25.4 us (22%)
  waiting for transfers between devices  7.83 us (7%)
  local copies, waits for them, and re-layouts  1.25 us (1%)
    all_to_all x1, blocking collectives, body(): lax.all_to_all(outgoing, 'lon', 0, 0, axis_index_groups=groups, tiled=True)  26.8 us
    ppermute x1, starting transfers between devices, body(): lax.ppermute(jnp.where(even, below, above), 'lon', swaps(lambda i: i + 1,...  22.4 us
    all_to_all x1, blocking collectives, body(): lax.all_to_all(attended.reshape(HEADS, half, 128), 'lon', 0, 0, axis_inde...  21.9 us
    pallas_call x6, Pallas kernels, attend(): pl.pallas_call(functools.partial(attention_kernel, first, final, [len(pie...  13.4 us
    pallas_call x1, Pallas kernels, body(): pl.pallas_call(conv_kernel, out_shape=(jax.ShapeDtypeStruct((count, CB),...  6.42 us
    pallas_call x1, Pallas kernels, body(): pl.pallas_call(middle_kernel, out_shape=(jax.ShapeDtypeStruct((3, cols, s...  4.52 us
    ppermute x2, starting transfers between devices, next_swap(): return lax.ppermute(value, 'lon', swaps(lambda i: i + 1, residues, HEADS))  3.66 us
    ppermute x2, waiting for transfers between devices, next_swap(): return lax.ppermute(value, 'lon', swaps(lambda i: i + 1, residues, HEADS))  3.35 us
  transfers between devices with their start and end apart: 12, of which 4 were waited for; matrix products, arithmetic and copies ran while one was open for 0% of the time, Pallas kernels for 14%

profile of v4, /device:TPU:40, one launch (start us, length us, event | category | flops | bytes accessed | tf_op | source)
XLA Modules:
  0.0 113.8 jit_solution(4815424560040903720)
XLA Ops:
  0.0 1.1 %copy.13 = bf16[128,8,256]{2,0,1:T(8,128)(2,1)S(1)} copy(bf16[128,8,256]{2,1,0:T(8,128)(2,1)} %param.6) | data formatting | bytes 1048576 | tf_op args[0]
  1.2 0.1 collective-permute-start
  1.4 1.1 collective-permute-done
  2.5 0.1 select_bitcast_fusion
  2.6 2.9 %collective-permute-start.1 = (bf16[3,131,256]{2,1,0:T(8,128)(2,1)S(1)}, bf16[3,131,256]{2,1,0:T(8,128)(2,1)S(1)}, u32[]{:S(2)}, u32[]{:S(2)}) collective-permute-start(bf16[3,131,256]{2,1,0:T(8,128)(2,1)S(1)} %get-tuple-element.46), channel_id=1, source_target_pairs={{0,2},{2,0},{4,6},{6,4},{8,10},{10,8},{12,14},{14,12},{16,18},{18,... | collective-permute-start | bytes 603656 | tf_op jit(solution)/shard_map/ppermute | solution.py:334
  5.5 22.4 %collective-permute-start.2 = (bf16[3,131,256]{2,1,0:T(8,128)(2,1)S(1)}, bf16[3,131,256]{2,1,0:T(8,128)(2,1)S(1)}, u32[]{:S(2)}, u32[]{:S(2)}) collective-permute-start(bf16[3,131,256]{2,1,0:T(8,128)(2,1)S(1)} %get-tuple-element.45), channel_id=1, source_target_pairs={{2,4},{4,2},{6,8},{8,6},{10,12},{12,10},{14,16},{16,14},{18,20},{2... | collective-permute-start | bytes 603656 | tf_op jit(solution)/shard_map/ppermute | solution.py:335
  27.8 0.1 pad_add_fusion.lat_ref
  27.9 0.0 copy-start.1
  27.9 4.5 %middle.1 = (bf16[3,8,144,256]{3,2,1,0:T(8,128)(2,1)S(1)}, bf16[3,2,64,512]{3,2,1,0:T(8,128)(2,1)S(1)}, bf16[2304,512]{1,0:T(8,128)(2,1)S(1)}, bf16[4608,512]{1,0:T(8,128)(2,1)S(1)}, bf16[512,3072]{1,0:T(8,128)(2,1)S(1)}) custom-call(s32[3]{0:T(128)S(1)} %pad_add_fusion.lat_ref, bf16[8,128,256]{2,1,0:T(8,128)(2,1)S(1)} %bitcast.15, ...), custom_call_target="tpu_custom_call" | custom-call | tf_op jit(solution)/shard_map/middle/pallas_call | solution.py:353
  32.4 0.0 collective-permute-done.1.pair_ref
  32.4 0.9 collective-permute-done.2.next_ref
  33.3 0.0 copy-done.1
  33.3 6.4 %convs.1 = (f32[64,512]{1,0:T(8,128)S(1)}, bf16[16,96,128]{2,1,0:T(8,128)(2,1)S(1)}) custom-call(s32[3]{0:T(128)S(1)} %pad_add_fusion.lat_ref, bf16[3,8,144,256]{3,2,1,0:T(8,128)(2,1)S(1)} %get-tuple-element.23.shifted, bf16[3,2,64,512]{3,2,1,0:T(8,128)(2,1)S(1)} %get-tuple-element.24.ready_mid, bf16[2304,512]{1,0:T(8,128)(2,1)S(1)} %get-tuple-element.25.conv_a_ref, ...), custom_call_target="tpu_custom_call" | custom-call | tf_op jit(solution)/shard_map/convs/pallas_call | solution.py:370
  39.8 26.8 %all_to_all.10 = bf16[16,96,128]{2,1,0:T(8,128)(2,1)S(1)} all-to-all(bf16[16,96,128]{2,1,0:T(8,128)(2,1)S(1)} %get-tuple-element.28), channel_id=1, replica_groups={{0,2,4,6,8,10,12,14,16,18,20,22,24,26,28,30},{32,34,36,38,40,42,44,46,4..., dimensions={0} | all-to-all | bytes 786432 | tf_op jit(solution)/shard_map/all_to_all | solution.py:392
  66.6 2.8 %collective-permute-start.3 = (bf16[1024,128]{1,0:T(8,128)(2,1)S(1)}, bf16[1024,128]{1,0:T(8,128)(2,1)S(1)}, u32[]{:S(2)}, u32[]{:S(2)}) collective-permute-start(bf16[1024,128]{1,0:T(8,128)(2,1)S(1)} %bitcast.16), channel_id=1, source_target_pairs={{32,64},{64,32},{34,66},{66,34},{36,68},{68,36},{38,70},{70,38},{4... | collective-permute-start | bytes 786440 | tf_op jit(solution)/shard_map/ppermute | solution.py:403
  69.4 0.0 collective-permute-start.6
  69.4 0.0 collective-permute-start.11
  69.4 1.6 %attention.6 = (bf16[2,512,128]{2,1,0:T(8,128)(2,1)S(1)}, f32[2,512,128]{2,1,0:T(8,128)S(1)}, f32[2,512,128]{2,1,0:T(8,128)S(1)}) custom-call(bf16[512,128]{1,0:T(8,128)(2,1)S(1)} %bitcast.21, bf16[1024,128]{1,0:T(8,128)(2,1)S(1)} %bitcast.19), custom_call_target="tpu_custom_call" | custom-call | flops 1073741824 | bytes 4194304 | tf_op jit(solution)/shard_map/attention/pallas_call | solution.py:272
  71.0 3.3 %collective-permute-done.3.refs_2_ = bf16[1024,128]{1,0:T(8,128)(2,1)S(1)} collective-permute-done((bf16[1024,128]{1,0:T(8,128)(2,1)S(1)}, bf16[1024,128]{1,0:T(8,128)(2,1)S(1)}, u32[]{:S(2)}, u32[]{:S(2)}) %collective-permute-start.3) | collective-permute-done | bytes 262176 | tf_op jit(solution)/shard_map/ppermute | solution.py:403
  74.3 0.1 collective-permute-start.4
  74.5 2.5 %collective-permute-done.6.refs_1_ = bf16[1024,128]{1,0:T(8,128)(2,1)S(1)} collective-permute-done((bf16[1024,128]{1,0:T(8,128)(2,1)S(1)}, bf16[1024,128]{1,0:T(8,128)(2,1)S(1)}, u32[]{:S(2)}, u32[]{:S(2)}) %collective-permute-start.6) | collective-permute-done | bytes 262176 | tf_op jit(solution)/shard_map/ppermute | solution.py:400
  76.9 0.9 collective-permute-start.7
  77.8 0.0 collective-permute-start.10
  77.8 0.5 collective-permute-start.9
  78.4 0.0 collective-permute-done.11.refs_1_
  78.4 1.8 %attention.7 = (f32[2,512,128]{2,1,0:T(8,128)S(1)}, f32[2,512,128]{2,1,0:T(8,128)S(1)}) custom-call(bf16[2,512,128]{2,1,0:T(8,128)(2,1)S(1)} %get-tuple-element.29.refs_0_, bf16[1024,128]{1,0:T(8,128)(2,1)S(1)} %collective-permute-done.11.refs_1_, f32[2,512,128]{2,1,0:T(8,128)S(1)} %get-tuple-element.30.refs_2_, f32[2,512,128]{2,1,0:T(8,128)S(1)} %get-tuple-element.31.refs_3_), custom_call_target="tpu_custom_call" | custom-call | flops 1073741824 | bytes 4194304 | tf_op jit(solution)/shard_map/attention/pallas_call | solution.py:272
  80.2 3.1 %attention.8 = (f32[2,512,128]{2,1,0:T(8,128)S(1)}, f32[2,512,128]{2,1,0:T(8,128)S(1)}) custom-call(bf16[2,512,128]{2,1,0:T(8,128)(2,1)S(1)} %get-tuple-element.29.refs_0_, bf16[1024,128]{1,0:T(8,128)(2,1)S(1)} %collective-permute-done.6.refs_1_, bf16[1024,128]{1,0:T(8,128)(2,1)S(1)} %collective-permute-done.3.refs_2_, ...), custom_call_target="tpu_custom_call" | custom-call | flops 2147483648 | bytes 4194304 | tf_op jit(solution)/shard_map/attention/pallas_call | solution.py:272
  83.2 0.0 collective-permute-done.4.refs_1_
  83.2 0.1 collective-permute-start.5
  83.4 0.0 collective-permute-done.7.refs_2_
  83.4 0.5 collective-permute-start.8
  83.9 0.0 collective-permute-done.10.refs_2_
  83.9 0.0 collective-permute-done.9.refs_1_
  83.9 3.1 %attention.9 = (f32[2,512,128]{2,1,0:T(8,128)S(1)}, f32[2,512,128]{2,1,0:T(8,128)S(1)}) custom-call(bf16[2,512,128]{2,1,0:T(8,128)(2,1)S(1)} %get-tuple-element.29.refs_0_, bf16[1024,128]{1,0:T(8,128)(2,1)S(1)} %collective-permute-done.9.refs_1_, bf16[1024,128]{1,0:T(8,128)(2,1)S(1)} %collective-permute-done.10.refs_2_, ...), custom_call_target="tpu_custom_call" | custom-call | flops 2147483648 | bytes 4194304 | tf_op jit(solution)/shard_map/attention/pallas_call | solution.py:272
  87.0 0.0 copy-start
  87.0 1.8 %attention.10 = (f32[2,512,128]{2,1,0:T(8,128)S(1)}, f32[2,512,128]{2,1,0:T(8,128)S(1)}) custom-call(bf16[2,512,128]{2,1,0:T(8,128)(2,1)S(1)} %get-tuple-element.29.refs_0_, bf16[512,128]{1,0:T(8,128)(2,1)S(1)} %collective-permute-done.4.refs_1_, bf16[512,128]{1,0:T(8,128)(2,1)S(1)} %collective-permute-done.7.refs_2_, ...), custom_call_target="tpu_custom_call" | custom-call | flops 1073741824 | bytes 4194304 | tf_op jit(solution)/shard_map/attention/pallas_call | solution.py:272
  88.8 0.0 collective-permute-done.5.refs_1_
  88.8 0.0 collective-permute-done.8.refs_2_
  88.8 2.0 %attention.11 = bf16[512,128]{1,0:T(8,128)(2,1)S(1)} custom-call(bf16[2,512,128]{2,1,0:T(8,128)(2,1)S(1)} %get-tuple-element.29.refs_0_, bf16[512,128]{1,0:T(8,128)(2,1)S(1)} %collective-permute-done.5.refs_1_, bf16[512,128]{1,0:T(8,128)(2,1)S(1)} %collective-permute-done.8.refs_2_, f32[2,512,128]{2,1,0:T(8,128)S(1)} %get-tuple-element.38.refs_3_, ...), custom_call_target="tpu_custom_call" | custom-call | flops 1073741824 | bytes 4194304 | tf_op jit(solution)/shard_map/attention/pallas_call | solution.py:272
  90.9 21.9 %all_to_all.11.back_ref = bf16[16,32,128]{2,1,0:T(8,128)(2,1)S(1)} all-to-all(bf16[16,32,128]{2,1,0:T(8,128)(2,1)S(1)} %bitcast.20), channel_id=1, replica_groups={{0,2,4,6,8,10,12,14,16,18,20,22,24,26,28,30},{32,34,36,38,40,42,44,46,4..., dimensions={0} | all-to-all | bytes 262144 | tf_op jit(solution)/shard_map/all_to_all | solution.py:421
  112.8 0.0 copy-done
  112.8 1.1 mix.1
  (7 shorter events, 0.1 us)
Async XLA Ops:
  1.2 1.3 %collective-permute-start = (bf16[3,8,256]{2,0,1:T(4,128)(2,1)S(1)}, bf16[3,8,256]{2,0,1:T(4,128)(2,1)S(1)}, u32[]{:S(2)}, u32[]{:S(2)}) collective-permute-start(bf16[3,8,256]{2,0,1:T(4,128)(2,1)S(1)} %constant_dynamic-slice_fusion), channel_id=1, source_target_pairs={{0,1},{1,0},{2,3},{3,2},{4,5},{5,4},{6,7},{7,6},{8,9},{9,8},{10,11... | collective-permute-start | bytes 36872 | tf_op jit(solution)/shard_map/ppermute | solution.py:325
  2.6 29.9 %collective-permute-start.1 = (bf16[3,131,256]{2,1,0:T(8,128)(2,1)S(1)}, bf16[3,131,256]{2,1,0:T(8,128)(2,1)S(1)}, u32[]{:S(2)}, u32[]{:S(2)}) collective-permute-start(bf16[3,131,256]{2,1,0:T(8,128)(2,1)S(1)} %get-tuple-element.46), channel_id=1, source_target_pairs={{0,2},{2,0},{4,6},{6,4},{8,10},{10,8},{12,14},{14,12},{16,18},{18,... | collective-permute-start | bytes 603656 | tf_op jit(solution)/shard_map/ppermute | solution.py:334
  5.5 27.9 %collective-permute-start.2 = (bf16[3,131,256]{2,1,0:T(8,128)(2,1)S(1)}, bf16[3,131,256]{2,1,0:T(8,128)(2,1)S(1)}, u32[]{:S(2)}, u32[]{:S(2)}) collective-permute-start(bf16[3,131,256]{2,1,0:T(8,128)(2,1)S(1)} %get-tuple-element.45), channel_id=1, source_target_pairs={{2,4},{4,2},{6,8},{8,6},{10,12},{12,10},{14,16},{16,14},{18,20},{2... | collective-permute-start | bytes 603656 | tf_op jit(solution)/shard_map/ppermute | solution.py:335
  27.9 5.4 %copy-start.1 = (f32[512]{0:T(512)S(1)}, f32[512]{0:T(512)}, u32[]{:S(2)}) copy-start(f32[512]{0:T(512)} %param.9) | copy-start | bytes 6148
  66.6 7.7 %collective-permute-start.3 = (bf16[1024,128]{1,0:T(8,128)(2,1)S(1)}, bf16[1024,128]{1,0:T(8,128)(2,1)S(1)}, u32[]{:S(2)}, u32[]{:S(2)}) collective-permute-start(bf16[1024,128]{1,0:T(8,128)(2,1)S(1)} %bitcast.16), channel_id=1, source_target_pairs={{32,64},{64,32},{34,66},{66,34},{36,68},{68,36},{38,70},{70,38},{4... | collective-permute-start | bytes 786440 | tf_op jit(solution)/shard_map/ppermute | solution.py:403
  69.4 7.6 %collective-permute-start.6 = (bf16[1024,128]{1,0:T(8,128)(2,1)S(1)}, bf16[1024,128]{1,0:T(8,128)(2,1)S(1)}, u32[]{:S(2)}, u32[]{:S(2)}) collective-permute-start(bf16[1024,128]{1,0:T(8,128)(2,1)S(1)} %bitcast.17), channel_id=1, source_target_pairs={{0,32},{32,0},{2,34},{34,2},{4,36},{36,4},{6,38},{38,6},{8,40},{40... | collective-permute-start | bytes 786440 | tf_op jit(solution)/shard_map/ppermute | solution.py:400
  69.4 9.0 %collective-permute-start.11 = (bf16[1024,128]{1,0:T(8,128)(2,1)S(1)}, bf16[1024,128]{1,0:T(8,128)(2,1)S(1)}, u32[]{:S(2)}, u32[]{:S(2)}) collective-permute-start(bf16[1024,128]{1,0:T(8,128)(2,1)S(1)} %bitcast.18), channel_id=1, source_target_pairs={{0,1},{1,0},{2,3},{3,2},{4,5},{5,4},{6,7},{7,6},{8,9},{9,8},{10,11... | collective-permute-start | bytes 786440 | tf_op jit(solution)/shard_map/ppermute | solution.py:397
  74.3 8.9 %collective-permute-start.4 = (bf16[512,128]{1,0:T(8,128)(2,1)S(1)}, bf16[512,128]{1,0:T(8,128)(2,1)S(1)}, u32[]{:S(2)}, u32[]{:S(2)}) collective-permute-start(bf16[512,128]{1,0:T(8,128)(2,1)S(1)} %slice.38), channel_id=1, source_target_pairs={{0,32},{32,0},{2,34},{34,2},{4,36},{36,4},{6,38},{38,6},{8,40},{40... | collective-permute-start | bytes 393224 | tf_op jit(solution)/shard_map/ppermute | solution.py:400
  76.9 6.5 %collective-permute-start.7 = (bf16[512,128]{1,0:T(8,128)(2,1)S(1)}, bf16[512,128]{1,0:T(8,128)(2,1)S(1)}, u32[]{:S(2)}, u32[]{:S(2)}) collective-permute-start(bf16[512,128]{1,0:T(8,128)(2,1)S(1)} %slice.39), channel_id=1, source_target_pairs={{32,64},{64,32},{34,66},{66,34},{36,68},{68,36},{38,70},{70,38},{4... | collective-permute-start | bytes 393224 | tf_op jit(solution)/shard_map/ppermute | solution.py:403
  77.8 6.0 %collective-permute-start.10 = (bf16[1024,128]{1,0:T(8,128)(2,1)S(1)}, bf16[1024,128]{1,0:T(8,128)(2,1)S(1)}, u32[]{:S(2)}, u32[]{:S(2)}) collective-permute-start(bf16[1024,128]{1,0:T(8,128)(2,1)S(1)} %collective-permute-done.3.refs_2_), channel_id=1, source_target_pairs={{0,1},{1,0},{2,3},{3,2},{4,5},{5,4},{6,7},{7,6},{8,9},{9,8},{10,11... | collective-permute-start | bytes 786440 | tf_op jit(solution)/shard_map/ppermute | solution.py:397
  77.8 6.0 %collective-permute-start.9 = (bf16[1024,128]{1,0:T(8,128)(2,1)S(1)}, bf16[1024,128]{1,0:T(8,128)(2,1)S(1)}, u32[]{:S(2)}, u32[]{:S(2)}) collective-permute-start(bf16[1024,128]{1,0:T(8,128)(2,1)S(1)} %collective-permute-done.6.refs_1_), channel_id=1, source_target_pairs={{0,1},{1,0},{2,3},{3,2},{4,5},{5,4},{6,7},{7,6},{8,9},{9,8},{10,11... | collective-permute-start | bytes 786440 | tf_op jit(solution)/shard_map/ppermute | solution.py:397
  83.2 5.5 %collective-permute-start.5 = (bf16[512,128]{1,0:T(8,128)(2,1)S(1)}, bf16[512,128]{1,0:T(8,128)(2,1)S(1)}, u32[]{:S(2)}, u32[]{:S(2)}) collective-permute-start(bf16[512,128]{1,0:T(8,128)(2,1)S(1)} %collective-permute-done.4.refs_1_), channel_id=1, source_target_pairs={{0,1},{1,0},{2,3},{3,2},{4,5},{5,4},{6,7},{7,6},{8,9},{9,8},{10,11... | collective-permute-start | bytes 393224 | tf_op jit(solution)/shard_map/ppermute | solution.py:397
  83.4 5.4 %collective-permute-start.8 = (bf16[512,128]{1,0:T(8,128)(2,1)S(1)}, bf16[512,128]{1,0:T(8,128)(2,1)S(1)}, u32[]{:S(2)}, u32[]{:S(2)}) collective-permute-start(bf16[512,128]{1,0:T(8,128)(2,1)S(1)} %collective-permute-done.7.refs_2_), channel_id=1, source_target_pairs={{0,1},{1,0},{2,3},{3,2},{4,5},{5,4},{6,7},{7,6},{8,9},{9,8},{10,11... | collective-permute-start | bytes 393224 | tf_op jit(solution)/shard_map/ppermute | solution.py:397
  87.0 25.8 %copy-start = (bf16[1024,512]{1,0:T(8,128)(2,1)S(1)}, bf16[1024,512]{1,0:T(8,128)(2,1)}, u32[]{:S(2)}) copy-start(bf16[1024,512]{1,0:T(8,128)(2,1)} %weight_ref.1) | copy-start | bytes 3145732

commit v5 on v4

--- a/solution.py
+++ b/solution.py
@@ -133,7 +133,7 @@
             return shifted[a, w - REACH]
         return high[a, w - REACH - cols]
 
-    for at, group in ((0, (0, 1)), (2, (pooled_cols - 2, pooled_cols - 1))):
+    for at, group in ((0, (0, 1, pooled_cols - 2, pooled_cols - 1)),):
         pairs = first_level(column, [2 * c for c in group], conv_a_ref[...], span)
         for n, pair in enumerate(pairs):
             store_pair(pool_side, at + n, pair, rows, lat, last)
@@ -408,11 +408,12 @@
     own_other = other(own)
     held = attend(queries, [(own_other,)], held, False)
     middle = own.shape[0] // 2
-    far_a = pair_swap(near_back[:middle])
     far_b = next_swap(near[middle:])
     near_other = other(near)
+    held = attend(queries, [(near,)], held, False)
+    far_a = pair_swap(near_back[:middle])
     near_back_other = other(near_back)
-    held = attend(queries, [(near,), (near_back,)], held, False)
+    held = attend(queries, [(near_back,)], held, False)
     held = attend(queries, [(near_other,), (near_back_other,)], held, False)
     far_a_other = other(far_a)
     far_b_other = other(far_b)

time: 114 us -> 115 us (level)
    pallas_call x6 -> x7, Pallas kernels: 13.4 us -> 13.9 us  [attend(): pl.pallas_call(functools.partial(attention_kernel, first, final, [len(pie...]
where the time goes in v5:
time: 115 us; the launch traced here: 114 us
  blocking collectives  48.7 us (42%)
  starting transfers between devices  30.3 us (26%)
  Pallas kernels  25.8 us (22%)
  waiting for transfers between devices  7.82 us (7%)
  local copies, waits for them, and re-layouts  1.25 us (1%)
    all_to_all x1, blocking collectives, body(): lax.all_to_all(outgoing, 'lon', 0, 0, axis_index_groups=groups, tiled=True)  26.8 us
    ppermute x1, starting transfers between devices, body(): lax.ppermute(jnp.where(even, below, above), 'lon', swaps(lambda i: i + 1,...  22.4 us
    all_to_all x1, blocking collectives, body(): lax.all_to_all(attended.reshape(HEADS, half, 128), 'lon', 0, 0, axis_inde...  21.9 us
    pallas_call x7, Pallas kernels, attend(): pl.pallas_call(functools.partial(attention_kernel, first, final, [len(pie...  13.9 us
    pallas_call x1, Pallas kernels, body(): pl.pallas_call(conv_kernel, out_shape=(jax.ShapeDtypeStruct((count, CB),...  6.33 us
    pallas_call x1, Pallas kernels, body(): pl.pallas_call(middle_kernel, out_shape=(jax.ShapeDtypeStruct((3, cols, s...  4.52 us
    ppermute x2, starting transfers between devices, next_swap(): return lax.ppermute(value, 'lon', swaps(lambda i: i + 1, residues, HEADS))  3.66 us
    ppermute x2, waiting for transfers between devices, next_swap(): return lax.ppermute(value, 'lon', swaps(lambda i: i + 1, residues, HEADS))  3.33 us
  transfers between devices with their start and end apart: 12, of which 4 were waited for; matrix products, arithmetic and copies ran while one was open for 0% of the time, Pallas kernels for 14%

profile of v5, /device:TPU:40, one launch (start us, length us, event | category | flops | bytes accessed | tf_op | source)
XLA Modules:
  0.0 114.3 jit_solution(11262233174736997553)
XLA Ops:
  0.0 1.1 copy.13
  1.2 0.1 collective-permute-start
  1.4 1.1 collective-permute-done
  2.5 0.1 select_bitcast_fusion
  2.6 2.9 %collective-permute-start.1 = (bf16[3,131,256]{2,1,0:T(8,128)(2,1)S(1)}, bf16[3,131,256]{2,1,0:T(8,128)(2,1)S(1)}, u32[]{:S(2)}, u32[]{:S(2)}) collective-permute-start(bf16[3,131,256]{2,1,0:T(8,128)(2,1)S(1)} %get-tuple-element.50), channel_id=1, source_target_pairs={{0,2},{2,0},{4,6},{6,4},{8,10},{10,8},{12,14},{14,12},{16,18},{18,... | collective-permute-start | bytes 603656 | tf_op jit(solution)/shard_map/ppermute | solution.py:334
  5.5 22.4 %collective-permute-start.2 = (bf16[3,131,256]{2,1,0:T(8,128)(2,1)S(1)}, bf16[3,131,256]{2,1,0:T(8,128)(2,1)S(1)}, u32[]{:S(2)}, u32[]{:S(2)}) collective-permute-start(bf16[3,131,256]{2,1,0:T(8,128)(2,1)S(1)} %get-tuple-element.49), channel_id=1, source_target_pairs={{2,4},{4,2},{6,8},{8,6},{10,12},{12,10},{14,16},{16,14},{18,20},{2... | collective-permute-start | bytes 603656 | tf_op jit(solution)/shard_map/ppermute | solution.py:335
  27.8 0.1 pad_add_fusion.lat_ref
  27.9 0.0 copy-start.1
  27.9 4.5 %middle.1 = (bf16[3,8,144,256]{3,2,1,0:T(8,128)(2,1)S(1)}, bf16[3,2,64,512]{3,2,1,0:T(8,128)(2,1)S(1)}, bf16[2304,512]{1,0:T(8,128)(2,1)S(1)}, bf16[4608,512]{1,0:T(8,128)(2,1)S(1)}, bf16[512,3072]{1,0:T(8,128)(2,1)S(1)}) custom-call(s32[3]{0:T(128)S(1)} %pad_add_fusion.lat_ref, bf16[8,128,256]{2,1,0:T(8,128)(2,1)S(1)} %bitcast.15, ...), custom_call_target="tpu_custom_call" | custom-call | tf_op jit(solution)/shard_map/middle/pallas_call | solution.py:353
  32.4 0.0 collective-permute-done.1.pair_ref
  32.4 0.9 collective-permute-done.2.next_ref
  33.3 0.0 copy-done.1
  33.3 6.3 %convs.1 = (f32[64,512]{1,0:T(8,128)S(1)}, bf16[16,96,128]{2,1,0:T(8,128)(2,1)S(1)}) custom-call(s32[3]{0:T(128)S(1)} %pad_add_fusion.lat_ref, bf16[3,8,144,256]{3,2,1,0:T(8,128)(2,1)S(1)} %get-tuple-element.25.shifted, bf16[3,2,64,512]{3,2,1,0:T(8,128)(2,1)S(1)} %get-tuple-element.26.ready_mid, bf16[2304,512]{1,0:T(8,128)(2,1)S(1)} %get-tuple-element.27.conv_a_ref, ...), custom_call_target="tpu_custom_call" | custom-call | tf_op jit(solution)/shard_map/convs/pallas_call | solution.py:370
  39.7 26.8 %all_to_all.10 = bf16[16,96,128]{2,1,0:T(8,128)(2,1)S(1)} all-to-all(bf16[16,96,128]{2,1,0:T(8,128)(2,1)S(1)} %get-tuple-element.30), channel_id=1, replica_groups={{0,2,4,6,8,10,12,14,16,18,20,22,24,26,28,30},{32,34,36,38,40,42,44,46,4..., dimensions={0} | all-to-all | bytes 786432 | tf_op jit(solution)/shard_map/all_to_all | solution.py:392
  66.5 2.8 %collective-permute-start.3 = (bf16[1024,128]{1,0:T(8,128)(2,1)S(1)}, bf16[1024,128]{1,0:T(8,128)(2,1)S(1)}, u32[]{:S(2)}, u32[]{:S(2)}) collective-permute-start(bf16[1024,128]{1,0:T(8,128)(2,1)S(1)} %bitcast.16), channel_id=1, source_target_pairs={{32,64},{64,32},{34,66},{66,34},{36,68},{68,36},{38,70},{70,38},{4... | collective-permute-start | bytes 786440 | tf_op jit(solution)/shard_map/ppermute | solution.py:403
  69.3 0.0 collective-permute-start.6
  69.3 0.0 collective-permute-start.11
  69.3 1.6 %attention.7 = (bf16[2,512,128]{2,1,0:T(8,128)(2,1)S(1)}, f32[2,512,128]{2,1,0:T(8,128)S(1)}, f32[2,512,128]{2,1,0:T(8,128)S(1)}) custom-call(bf16[512,128]{1,0:T(8,128)(2,1)S(1)} %bitcast.21, bf16[1024,128]{1,0:T(8,128)(2,1)S(1)} %bitcast.19), custom_call_target="tpu_custom_call" | custom-call | flops 1073741824 | bytes 4194304 | tf_op jit(solution)/shard_map/attention/pallas_call | solution.py:272
  70.9 3.3 %collective-permute-done.3.refs_1_ = bf16[1024,128]{1,0:T(8,128)(2,1)S(1)} collective-permute-done((bf16[1024,128]{1,0:T(8,128)(2,1)S(1)}, bf16[1024,128]{1,0:T(8,128)(2,1)S(1)}, u32[]{:S(2)}, u32[]{:S(2)}) %collective-permute-start.3) | collective-permute-done | bytes 262176 | tf_op jit(solution)/shard_map/ppermute | solution.py:403
  74.2 0.1 collective-permute-start.4
  74.4 2.5 %collective-permute-done.6.refs_1_ = bf16[1024,128]{1,0:T(8,128)(2,1)S(1)} collective-permute-done((bf16[1024,128]{1,0:T(8,128)(2,1)S(1)}, bf16[1024,128]{1,0:T(8,128)(2,1)S(1)}, u32[]{:S(2)}, u32[]{:S(2)}) %collective-permute-start.6) | collective-permute-done | bytes 262176 | tf_op jit(solution)/shard_map/ppermute | solution.py:400
  76.9 0.9 collective-permute-start.7
  77.8 0.0 collective-permute-start.10
  77.8 0.5 collective-permute-start.9
  78.3 0.0 collective-permute-done.11.refs_1_
  78.3 1.8 %attention.8 = (f32[2,512,128]{2,1,0:T(8,128)S(1)}, f32[2,512,128]{2,1,0:T(8,128)S(1)}) custom-call(bf16[2,512,128]{2,1,0:T(8,128)(2,1)S(1)} %get-tuple-element.31.refs_0_, bf16[1024,128]{1,0:T(8,128)(2,1)S(1)} %collective-permute-done.11.refs_1_, f32[2,512,128]{2,1,0:T(8,128)S(1)} %get-tuple-element.32.refs_2_, f32[2,512,128]{2,1,0:T(8,128)S(1)} %get-tuple-element.33.refs_3_), custom_call_target="tpu_custom_call" | custom-call | flops 1073741824 | bytes 4194304 | tf_op jit(solution)/shard_map/attention/pallas_call | solution.py:272
  80.1 1.8 %attention.9 = (f32[2,512,128]{2,1,0:T(8,128)S(1)}, f32[2,512,128]{2,1,0:T(8,128)S(1)}) custom-call(bf16[2,512,128]{2,1,0:T(8,128)(2,1)S(1)} %get-tuple-element.31.refs_0_, bf16[1024,128]{1,0:T(8,128)(2,1)S(1)} %collective-permute-done.6.refs_1_, f32[2,512,128]{2,1,0:T(8,128)S(1)} %get-tuple-element.34.refs_2_, f32[2,512,128]{2,1,0:T(8,128)S(1)} %get-tuple-element.35.refs_3_), custom_call_target="tpu_custom_call" | custom-call | flops 1073741824 | bytes 4194304 | tf_op jit(solution)/shard_map/attention/pallas_call | solution.py:272
  81.9 1.8 %attention.10 = (f32[2,512,128]{2,1,0:T(8,128)S(1)}, f32[2,512,128]{2,1,0:T(8,128)S(1)}) custom-call(bf16[2,512,128]{2,1,0:T(8,128)(2,1)S(1)} %get-tuple-element.31.refs_0_, bf16[1024,128]{1,0:T(8,128)(2,1)S(1)} %collective-permute-done.3.refs_1_, f32[2,512,128]{2,1,0:T(8,128)S(1)} %get-tuple-element.36.refs_2_, f32[2,512,128]{2,1,0:T(8,128)S(1)} %get-tuple-element.37.refs_3_), custom_call_target="tpu_custom_call" | custom-call | flops 1073741824 | bytes 4194304 | tf_op jit(solution)/shard_map/attention/pallas_call | solution.py:272
  83.7 0.0 collective-permute-done.4.refs_1_
  83.7 0.1 collective-permute-start.5
  83.9 0.0 collective-permute-done.7.refs_2_
  83.9 0.5 collective-permute-start.8
  84.3 0.0 collective-permute-done.10.refs_2_
  84.3 0.0 collective-permute-done.9.refs_1_
  84.4 3.1 %attention.11 = (f32[2,512,128]{2,1,0:T(8,128)S(1)}, f32[2,512,128]{2,1,0:T(8,128)S(1)}) custom-call(bf16[2,512,128]{2,1,0:T(8,128)(2,1)S(1)} %get-tuple-element.31.refs_0_, bf16[1024,128]{1,0:T(8,128)(2,1)S(1)} %collective-permute-done.9.refs_1_, bf16[1024,128]{1,0:T(8,128)(2,1)S(1)} %collective-permute-done.10.refs_2_, ...), custom_call_target="tpu_custom_call" | custom-call | flops 2147483648 | bytes 4194304 | tf_op jit(solution)/shard_map/attention/pallas_call | solution.py:272
  87.4 0.0 copy-start
  87.4 1.8 %attention.12 = (f32[2,512,128]{2,1,0:T(8,128)S(1)}, f32[2,512,128]{2,1,0:T(8,128)S(1)}) custom-call(bf16[2,512,128]{2,1,0:T(8,128)(2,1)S(1)} %get-tuple-element.31.refs_0_, bf16[512,128]{1,0:T(8,128)(2,1)S(1)} %collective-permute-done.4.refs_1_, bf16[512,128]{1,0:T(8,128)(2,1)S(1)} %collective-permute-done.7.refs_2_, ...), custom_call_target="tpu_custom_call" | custom-call | flops 1073741824 | bytes 4194304 | tf_op jit(solution)/shard_map/attention/pallas_call | solution.py:272
  89.3 0.0 collective-permute-done.5.refs_1_
  89.3 0.0 collective-permute-done.8.refs_2_
  89.3 2.0 %attention.13 = bf16[512,128]{1,0:T(8,128)(2,1)S(1)} custom-call(bf16[2,512,128]{2,1,0:T(8,128)(2,1)S(1)} %get-tuple-element.31.refs_0_, bf16[512,128]{1,0:T(8,128)(2,1)S(1)} %collective-permute-done.5.refs_1_, bf16[512,128]{1,0:T(8,128)(2,1)S(1)} %collective-permute-done.8.refs_2_, f32[2,512,128]{2,1,0:T(8,128)S(1)} %get-tuple-element.42.refs_3_, ...), custom_call_target="tpu_custom_call" | custom-call | flops 1073741824 | bytes 4194304 | tf_op jit(solution)/shard_map/attention/pallas_call | solution.py:272
  91.3 21.9 %all_to_all.11.back_ref = bf16[16,32,128]{2,1,0:T(8,128)(2,1)S(1)} all-to-all(bf16[16,32,128]{2,1,0:T(8,128)(2,1)S(1)} %bitcast.20), channel_id=1, replica_groups={{0,2,4,6,8,10,12,14,16,18,20,22,24,26,28,30},{32,34,36,38,40,42,44,46,4..., dimensions={0} | all-to-all | bytes 262144 | tf_op jit(solution)/shard_map/all_to_all | solution.py:422
  113.2 0.0 copy-done
  113.2 1.1 mix.1
  (7 shorter events, 0.1 us)
Async XLA Ops:
  1.2 1.3 %collective-permute-start = (bf16[3,8,256]{2,0,1:T(4,128)(2,1)S(1)}, bf16[3,8,256]{2,0,1:T(4,128)(2,1)S(1)}, u32[]{:S(2)}, u32[]{:S(2)}) collective-permute-start(bf16[3,8,256]{2,0,1:T(4,128)(2,1)S(1)} %constant_dynamic-slice_fusion), channel_id=1, source_target_pairs={{0,1},{1,0},{2,3},{3,2},{4,5},{5,4},{6,7},{7,6},{8,9},{9,8},{10,11... | collective-permute-start | bytes 36872 | tf_op jit(solution)/shard_map/ppermute | solution.py:325
  2.6 29.9 %collective-permute-start.1 = (bf16[3,131,256]{2,1,0:T(8,128)(2,1)S(1)}, bf16[3,131,256]{2,1,0:T(8,128)(2,1)S(1)}, u32[]{:S(2)}, u32[]{:S(2)}) collective-permute-start(bf16[3,131,256]{2,1,0:T(8,128)(2,1)S(1)} %get-tuple-element.50), channel_id=1, source_target_pairs={{0,2},{2,0},{4,6},{6,4},{8,10},{10,8},{12,14},{14,12},{16,18},{18,... | collective-permute-start | bytes 603656 | tf_op jit(solution)/shard_map/ppermute | solution.py:334
  5.5 27.9 %collective-permute-start.2 = (bf16[3,131,256]{2,1,0:T(8,128)(2,1)S(1)}, bf16[3,131,256]{2,1,0:T(8,128)(2,1)S(1)}, u32[]{:S(2)}, u32[]{:S(2)}) collective-permute-start(bf16[3,131,256]{2,1,0:T(8,128)(2,1)S(1)} %get-tuple-element.49), channel_id=1, source_target_pairs={{2,4},{4,2},{6,8},{8,6},{10,12},{12,10},{14,16},{16,14},{18,20},{2... | collective-permute-start | bytes 603656 | tf_op jit(solution)/shard_map/ppermute | solution.py:335
  27.9 5.4 %copy-start.1 = (f32[512]{0:T(512)S(1)}, f32[512]{0:T(512)}, u32[]{:S(2)}) copy-start(f32[512]{0:T(512)} %param.9) | copy-start | bytes 6148
  66.5 7.7 %collective-permute-start.3 = (bf16[1024,128]{1,0:T(8,128)(2,1)S(1)}, bf16[1024,128]{1,0:T(8,128)(2,1)S(1)}, u32[]{:S(2)}, u32[]{:S(2)}) collective-permute-start(bf16[1024,128]{1,0:T(8,128)(2,1)S(1)} %bitcast.16), channel_id=1, source_target_pairs={{32,64},{64,32},{34,66},{66,34},{36,68},{68,36},{38,70},{70,38},{4... | collective-permute-start | bytes 786440 | tf_op jit(solution)/shard_map/ppermute | solution.py:403
  69.3 7.6 %collective-permute-start.6 = (bf16[1024,128]{1,0:T(8,128)(2,1)S(1)}, bf16[1024,128]{1,0:T(8,128)(2,1)S(1)}, u32[]{:S(2)}, u32[]{:S(2)}) collective-permute-start(bf16[1024,128]{1,0:T(8,128)(2,1)S(1)} %bitcast.17), channel_id=1, source_target_pairs={{0,32},{32,0},{2,34},{34,2},{4,36},{36,4},{6,38},{38,6},{8,40},{40... | collective-permute-start | bytes 786440 | tf_op jit(solution)/shard_map/ppermute | solution.py:400
  69.3 9.0 %collective-permute-start.11 = (bf16[1024,128]{1,0:T(8,128)(2,1)S(1)}, bf16[1024,128]{1,0:T(8,128)(2,1)S(1)}, u32[]{:S(2)}, u32[]{:S(2)}) collective-permute-start(bf16[1024,128]{1,0:T(8,128)(2,1)S(1)} %bitcast.18), channel_id=1, source_target_pairs={{0,1},{1,0},{2,3},{3,2},{4,5},{5,4},{6,7},{7,6},{8,9},{9,8},{10,11... | collective-permute-start | bytes 786440 | tf_op jit(solution)/shard_map/ppermute | solution.py:397
  74.2 9.5 %collective-permute-start.4 = (bf16[512,128]{1,0:T(8,128)(2,1)S(1)}, bf16[512,128]{1,0:T(8,128)(2,1)S(1)}, u32[]{:S(2)}, u32[]{:S(2)}) collective-permute-start(bf16[512,128]{1,0:T(8,128)(2,1)S(1)} %slice.38), channel_id=1, source_target_pairs={{0,32},{32,0},{2,34},{34,2},{4,36},{36,4},{6,38},{38,6},{8,40},{40... | collective-permute-start | bytes 393224 | tf_op jit(solution)/shard_map/ppermute | solution.py:400
  76.9 7.0 %collective-permute-start.7 = (bf16[512,128]{1,0:T(8,128)(2,1)S(1)}, bf16[512,128]{1,0:T(8,128)(2,1)S(1)}, u32[]{:S(2)}, u32[]{:S(2)}) collective-permute-start(bf16[512,128]{1,0:T(8,128)(2,1)S(1)} %slice.39), channel_id=1, source_target_pairs={{32,64},{64,32},{34,66},{66,34},{36,68},{68,36},{38,70},{70,38},{4... | collective-permute-start | bytes 393224 | tf_op jit(solution)/shard_map/ppermute | solution.py:403
  77.8 6.6 %collective-permute-start.10 = (bf16[1024,128]{1,0:T(8,128)(2,1)S(1)}, bf16[1024,128]{1,0:T(8,128)(2,1)S(1)}, u32[]{:S(2)}, u32[]{:S(2)}) collective-permute-start(bf16[1024,128]{1,0:T(8,128)(2,1)S(1)} %collective-permute-done.3.refs_1_), channel_id=1, source_target_pairs={{0,1},{1,0},{2,3},{3,2},{4,5},{5,4},{6,7},{7,6},{8,9},{9,8},{10,11... | collective-permute-start | bytes 786440 | tf_op jit(solution)/shard_map/ppermute | solution.py:397
  77.8 6.6 %collective-permute-start.9 = (bf16[1024,128]{1,0:T(8,128)(2,1)S(1)}, bf16[1024,128]{1,0:T(8,128)(2,1)S(1)}, u32[]{:S(2)}, u32[]{:S(2)}) collective-permute-start(bf16[1024,128]{1,0:T(8,128)(2,1)S(1)} %collective-permute-done.6.refs_1_), channel_id=1, source_target_pairs={{0,1},{1,0},{2,3},{3,2},{4,5},{5,4},{6,7},{7,6},{8,9},{9,8},{10,11... | collective-permute-start | bytes 786440 | tf_op jit(solution)/shard_map/ppermute | solution.py:397
  83.7 5.5 %collective-permute-start.5 = (bf16[512,128]{1,0:T(8,128)(2,1)S(1)}, bf16[512,128]{1,0:T(8,128)(2,1)S(1)}, u32[]{:S(2)}, u32[]{:S(2)}) collective-permute-start(bf16[512,128]{1,0:T(8,128)(2,1)S(1)} %collective-permute-done.4.refs_1_), channel_id=1, source_target_pairs={{0,1},{1,0},{2,3},{3,2},{4,5},{5,4},{6,7},{7,6},{8,9},{9,8},{10,11... | collective-permute-start | bytes 393224 | tf_op jit(solution)/shard_map/ppermute | solution.py:397
  83.9 5.4 %collective-permute-start.8 = (bf16[512,128]{1,0:T(8,128)(2,1)S(1)}, bf16[512,128]{1,0:T(8,128)(2,1)S(1)}, u32[]{:S(2)}, u32[]{:S(2)}) collective-permute-start(bf16[512,128]{1,0:T(8,128)(2,1)S(1)} %collective-permute-done.7.refs_2_), channel_id=1, source_target_pairs={{0,1},{1,0},{2,3},{3,2},{4,5},{5,4},{6,7},{7,6},{8,9},{9,8},{10,11... | collective-permute-start | bytes 393224 | tf_op jit(solution)/shard_map/ppermute | solution.py:397
  87.4 25.8 %copy-start = (bf16[1024,512]{1,0:T(8,128)(2,1)S(1)}, bf16[1024,512]{1,0:T(8,128)(2,1)}, u32[]{:S(2)}) copy-start(bf16[1024,512]{1,0:T(8,128)(2,1)} %weight_ref.1) | copy-start | bytes 3145732
